TPU v7x, 128 devices: a whole 4x4x4 slice. The times are simulated.
128 devices in a mesh: row: 8 (over x, z_hi), col: 16 (over y, z_lo, core).
Axes of the slice: x: 4, y: 4, z: 4 (z_hi: 2, z_lo: 2; z = z_hi * 2 + z_lo), core: 2. Of those that a mesh axis runs over, the one named last changes fastest.
Arguments:
- pair_act: float32 [768, 768, 128], P('row', 'col'), may hold values from -6 to 6
- grad_out: float32 [768, 768, 128], P('row', 'col'), may hold values from -6 to 6
- residue_mask: int32 [768], replicated, may hold values from 0 to 1, as said below
- norm_gains: float32 [2, 128], replicated, may hold values from 0.25 to 1.75
- weights: float32 [6, 128, 128], replicated, may hold values from -0.5 to 0.5
Outputs:
- grad_pair: float32 [768, 768, 128], P('row', 'col')
- grad_weights: float32 [6, 128, 128], replicated
- grad_gains: float32 [2, 128], replicated
Inputs may be any that keep to these rules, and one draw needn't show every extreme that they name: `residue_mask`: the residues form four stretches of 192; in each stretch the valid residues are a prefix of at least 96 and fewer than 192 residues.
All inputs are finite; a program needn't handle non-finite values.
Results may differ from a plain program's by a relative error of at most 0.00009.
Values sent between devices are 32-bit elements; how exact they have to be, the bound alone decides.
A program may use at most 128 MiB of HBM per device.

v0:
```python
import jax
import jax.numpy as jnp
from jax import lax
from jax.sharding import PartitionSpec as P

epsilon = 1e-05
highest = lax.Precision.HIGHEST


def from_everyone(shard, axis):
    copies = jnp.broadcast_to(shard, (lax.axis_size(axis), *shard.shape))
    return lax.all_to_all(copies, axis, split_axis=0, concat_axis=0, tiled=True)


def of_everyone(shard, axis):
    everything = from_everyone(shard, axis)
    return jnp.sum(everything, axis=0)


def norm_parts(operand):
    average = jnp.mean(operand, axis=-1, keepdims=True)
    centered = operand - average
    inv_std = lax.rsqrt(jnp.mean(centered * centered, axis=-1, keepdims=True) + epsilon)
    return (centered * inv_std, inv_std)


def norm_back(grad_hat, normed, inv_std):
    first_mean = jnp.mean(grad_hat, axis=-1, keepdims=True)
    second_mean = jnp.mean(grad_hat * normed, axis=-1, keepdims=True)
    return inv_std * (grad_hat - first_mean - normed * second_mean)


def project(operand, weight):
    return jnp.einsum("ijc,cd->ijd", operand, weight, precision=highest)


def sigmoid(operand):
    return 1.0 / (1.0 + jnp.exp(-operand))


def channel_major(tiles):
    return jnp.transpose(tiles, (0, 3, 1, 2))


def arrange_direct(arrived, tile_rows, tile_cols):
    row_count = lax.axis_size("row")
    col_count = lax.axis_size("col")
    stack_count = arrived.shape[0]
    local_chans = arrived.shape[1]
    shaped = arrived.reshape(stack_count, local_chans, row_count, col_count, tile_rows, tile_cols)
    shaped = jnp.transpose(shaped, (0, 1, 2, 4, 3, 5))
    return shaped.reshape(stack_count, local_chans, row_count * tile_rows, col_count * tile_cols)


def split_direct(chan_stack, tile_rows, tile_cols):
    row_count = lax.axis_size("row")
    col_count = lax.axis_size("col")
    stack_count = chan_stack.shape[0]
    local_chans = chan_stack.shape[1]
    shaped = chan_stack.reshape(
        stack_count, local_chans, row_count, tile_rows, col_count, tile_cols
    )
    shaped = jnp.transpose(shaped, (0, 2, 4, 1, 3, 5))
    return shaped.reshape(stack_count, row_count * col_count, local_chans, tile_rows, tile_cols)


def back_positions(arrived, tile_rows, tile_cols):
    stack_count = arrived.shape[0]
    return jnp.transpose(arrived.reshape(stack_count, -1, tile_rows, tile_cols), (0, 2, 3, 1))


def acts_to_channels(stacked, tile_rows, tile_cols):
    arrived = lax.all_to_all(stacked, ("row", "col"), split_axis=1, concat_axis=2, tiled=True)
    result = arrange_direct(arrived, tile_rows, tile_cols)
    return result


def dtri_to_channels(stacked, tile_rows, tile_cols):
    arrived = lax.all_to_all(stacked, ("row", "col"), split_axis=1, concat_axis=2, tiled=True)
    result = arrange_direct(arrived, tile_rows, tile_cols)
    return result


def tri_to_positions(chan_stack, tile_rows, tile_cols):
    arrived = lax.all_to_all(
        split_direct(chan_stack, tile_rows, tile_cols),
        ("row", "col"),
        split_axis=1,
        concat_axis=1,
        tiled=True,
    )
    return back_positions(arrived, tile_rows, tile_cols)


def grads_to_positions(chan_stack, tile_rows, tile_cols):
    arrived = lax.all_to_all(
        split_direct(chan_stack, tile_rows, tile_cols),
        ("row", "col"),
        split_axis=1,
        concat_axis=1,
        tiled=True,
    )
    return back_positions(arrived, tile_rows, tile_cols)


def on_device(pair_act, grad_out, residue_mask, norm_gains, weights):
    tile_rows, tile_cols, channels = pair_act.shape
    residues = residue_mask.shape[0]
    row_mask = lax.dynamic_slice_in_dim(residue_mask, lax.axis_index("row") * tile_rows, tile_rows)
    col_mask = lax.dynamic_slice_in_dim(residue_mask, lax.axis_index("col") * tile_cols, tile_cols)
    pair_mask = (row_mask[:, None] * col_mask[None, :]).astype(jnp.float32)[:, :, None]
    pair_hat, inv_std = norm_parts(pair_act)
    normed = pair_hat * norm_gains[0]
    lin_a = project(normed, weights[0])
    sig_a = sigmoid(project(normed, weights[1]))
    lin_b = project(normed, weights[2])
    sig_b = sigmoid(project(normed, weights[3]))
    act_stack = jnp.stack([pair_mask * sig_a * lin_a, pair_mask * sig_b * lin_b])
    chan_acts = acts_to_channels(channel_major(act_stack), tile_rows, tile_cols)
    chan_tri = jnp.einsum("lik,ljk->lij", chan_acts[0], chan_acts[1], precision=highest)
    triangle = tri_to_positions(chan_tri[None], tile_rows, tile_cols)[0]
    tri_hat, tri_inv = norm_parts(triangle)
    tri_norm = tri_hat * norm_gains[1]
    lin_o = project(tri_norm, weights[5])
    sig_g = sigmoid(project(normed, weights[4]))
    d_out = grad_out * sig_g
    d_gate = grad_out * lin_o * sig_g * (1.0 - sig_g)
    d_norm = project(d_out, weights[5].T)
    d_tri = norm_back(d_norm * norm_gains[1], tri_hat, tri_inv)
    chan_dtri = dtri_to_channels(channel_major(d_tri[None]), tile_rows, tile_cols)[0]
    chan_da = jnp.einsum("lij,ljk->lik", chan_dtri, chan_acts[1], precision=highest)
    chan_db = jnp.einsum("lij,lik->ljk", chan_dtri, chan_acts[0], precision=highest)
    d_acts = grads_to_positions(jnp.stack([chan_da, chan_db]), tile_rows, tile_cols)
    d_lin_a = d_acts[0] * pair_mask * sig_a
    d_sig_a = d_acts[0] * pair_mask * lin_a * sig_a * (1.0 - sig_a)
    d_lin_b = d_acts[1] * pair_mask * sig_b
    d_sig_b = d_acts[1] * pair_mask * lin_b * sig_b * (1.0 - sig_b)
    grads_cat = jnp.concatenate([d_lin_a, d_sig_a, d_lin_b, d_sig_b, d_gate], axis=-1).reshape(
        -1, 5 * channels
    )
    weights_turned = jnp.transpose(weights[:5], (0, 2, 1)).reshape(5 * channels, channels)
    d_normed = jnp.dot(grads_cat, weights_turned, precision=highest).reshape(
        tile_rows, tile_cols, channels
    )
    flat_normed = normed.reshape(-1, channels)
    weight_part = jnp.einsum("pc,pd->cd", flat_normed, grads_cat, precision=highest)
    weight_part = jnp.transpose(weight_part.reshape(channels, 5, channels), (1, 0, 2)).reshape(
        5 * channels, channels
    )
    out_part = jnp.einsum(
        "pc,pd->cd", tri_norm.reshape(-1, channels), d_out.reshape(-1, channels), precision=highest
    )
    gain_one = jnp.sum(d_normed * pair_hat, axis=(0, 1))
    gain_two = jnp.sum(d_norm * tri_hat, axis=(0, 1))
    grad_pair = norm_back(d_normed * norm_gains[0], pair_hat, inv_std)
    combined = jnp.concatenate([weight_part, out_part, gain_one[None], gain_two[None]], axis=0)
    column_total = of_everyone(combined, "col")
    total = of_everyone(column_total, "row")
    scaled = total / residues
    grad_weights = scaled[: 6 * channels].reshape(6, channels, channels)
    grad_gains = scaled[6 * channels :]
    return (grad_pair, grad_weights, grad_gains)


def solution(mesh):
    return jax.shard_map(
        on_device,
        mesh=mesh,
        in_specs=(P("row", "col", None), P("row", "col", None), P(), P(), P()),
        out_specs=(P("row", "col", None), P(), P()),
        check_vma=False,
    )
```

profile of v0, /device:TPU:1, one launch (start us, length us, event | category | flops | bytes accessed | tf_op | source)
XLA Modules:
  0.0 582.4 jit_solution(5280849405233488929)
XLA Ops:
  0.7 2.5 reduce_sum.108
  6.2 2.0 add_divide_fusion.1
  8.3 3.4 add_divide_fusion.2
  11.7 3.4 fusion.29
  15.1 3.4 fusion.32
  20.1 3.5 multiply_bitcast_fusion.2
  23.6 2.5 maximum_bitcast_fusion
  26.1 6.3 %copy.82 = f32[2,128,96,48]{2,3,0,1:T(8,128)} copy(f32[2,128,96,48]{1,3,2,0:T(8,128)} %maximum_bitcast_fusion) | data formatting | bytes 9437184 | tf_op jit(solution)/shard_map/transpose | solution.py:42
  32.4 86.9 %all_to_all.38 = f32[2,128,96,48]{2,3,0,1:T(8,128)S(1)} all-to-all(f32[2,128,96,48]{2,3,0,1:T(8,128)} %copy.82), channel_id=1, replica_groups=mesh['row'=8,'col'=16] {'row','col'}, dimensions={1} | all-to-all | bytes 9437184 | tf_op jit(solution)/shard_map/all_to_all | solution.py:73
  119.9 2.3 fusion.42
  122.2 6.6 %copy.84 = f32[1,1,8,96,16,48]{5,4,3,2,1,0:T(8,128)} copy(f32[1,1,8,96,16,48]{3,5,4,2,0,1:T(8,128)} %get-tuple-element.9) | data formatting | bytes 4718592 | tf_op jit(solution)/shard_map/slice | solution.py:120
  128.8 6.0 %reshape.205 = f32[16,48,768,1]{2,1,0,3:T(8,128)} reshape(f32[1,1,8,96,16,48]{5,4,3,2,1,0:T(8,128)} %copy.84) | data formatting | bytes 4718592 | tf_op jit(solution)/shard_map/lik,ljk->lij/dot_general | solution.py:120
  134.9 10.5 %fusion.43 = f32[8,96,16,48]{1,3,2,0:T(8,128)} fusion(f32[8,96,768,1]{1,2,3,0:T(8,128)S(1)} %bitcast.202, f32[16,48,768,1]{2,1,0,3:T(8,128)} %reshape.205), kind=kOutput, calls=%fused_computation.81 | convolution fusion | flops 5435817984 | bytes 7077888 | tf_op jit(solution)/shard_map/lik,ljk->lij/dot_general | solution.py:120
  145.3 7.0 %all-to-all-start.1 = ((f32[1,128,1,96,48]{3,4,2,0,1:T(8,128)}), f32[1,128,1,96,48]{3,4,2,0,1:T(8,128)}, u32[]{:S(2)}, u32[]{:S(2)}) async-start(f32[1,128,1,96,48]{3,4,2,0,1:T(8,128)} %bitcast.205), calls=%async_computation.1 | async-start | bytes 6291456 | tf_op jit(solution)/shard_map/all_to_all | solution.py:85
  152.3 4.3 add_divide_fusion
  156.6 36.5 %all-to-all-done.1 = f32[1,128,1,96,48]{3,4,2,0,1:T(8,128)} async-done(((f32[1,128,1,96,48]{3,4,2,0,1:T(8,128)}), f32[1,128,1,96,48]{3,4,2,0,1:T(8,128)}, u32[]{:S(2)}, u32[]{:S(2)}) %all-to-all-start.1) | async-done | bytes 2359328 | tf_op jit(solution)/shard_map/all_to_all | solution.py:85
  193.2 2.5 copy.87
  198.1 4.2 multiply_reduce_fusion
  202.3 4.2 multiply_bitcast_fusion
  206.5 3.5 copy.88
  210.0 6.2 %all-to-all-start.2 = ((f32[1,128,96,48]{2,3,0,1:T(8,128)}), f32[1,128,96,48]{2,3,0,1:T(8,128)}, u32[]{:S(2)}, u32[]{:S(2)}) async-start(f32[1,128,96,48]{2,3,0,1:T(8,128)} %copy.88), calls=%async_computation.2 | async-start | bytes 6291456 | tf_op jit(solution)/shard_map/all_to_all | solution.py:79
  216.2 5.5 copy.89
  221.8 3.5 copy.92
  225.3 4.4 reshape.189
  229.7 4.4 reshape.192
  234.1 23.0 %all-to-all-done.2 = f32[1,128,96,48]{2,3,0,1:T(8,128)} async-done(((f32[1,128,96,48]{2,3,0,1:T(8,128)}), f32[1,128,96,48]{2,3,0,1:T(8,128)}, u32[]{:S(2)}, u32[]{:S(2)}) %all-to-all-start.2) | async-done | bytes 2359328 | tf_op jit(solution)/shard_map/all_to_all | solution.py:79
  257.0 5.4 copy.91
  262.5 4.6 reshape.190
  267.1 10.9 %convolution_bitcast_fusion.1 = f32[1,1,8,96,16,48]{3,5,4,2,1,0:T(8,128)S(1)} fusion(f32[8,96,768,1]{1,2,3,0:T(8,128)} %bitcast.80, f32[16,48,768,1]{2,1,0,3:T(8,128)} %bitcast.206), kind=kOutput, calls=%fused_computation.38 | convolution fusion | flops 5435817984 | bytes 7077888 | tf_op jit(solution)/shard_map/lij,ljk->lik/dot_general | solution.py:131
  278.1 8.2 %convolution_bitcast_fusion = f32[1,1,8,96,16,48]{3,5,4,2,1,0:T(8,128)S(1)} fusion(f32[8,96,768,1]{2,1,3,0:T(8,128)S(1)} %bitcast.208, f32[16,48,768,1]{2,1,0,3:T(8,128)S(1)} %bitcast.207), kind=kOutput, calls=%fused_computation.37 | convolution fusion | flops 5435817984 | bytes 7077888 | tf_op jit(solution)/shard_map/lij,lik->ljk/dot_general | solution.py:132
  286.9 3.6 copy.93
  290.5 5.7 all-to-all-start.3
  297.4 7.6 %fusion.20 = f32[128,128]{1,0:T(8,128)S(1)} fusion(f32[1,128,1,96,48]{1,4,3,2,0:T(8,128)S(1)} %copy.87, f32[128]{0:T(128)S(1)} %get-tuple-element.13, f32[96,48]{1,0:T(8,128)S(1)} %add_rsqrt_fusion, f32[96,48]{1,0:T(8,128)S(1)} %broadcast_multiply_fusion.5, f32[96,48,128]{2,1,0:T(8,128)} %param.6, f32[96,48,128]{2,1,0:T(8,128)} %add_divide_fusion), kind=kOutput, calls=%fused_computation.46 | convolution fusion | flops 908328960 | bytes 7180800 | tf_op jit(solution)/shard_map/pc,pd->cd/dot_general | solution.py:150
  305.0 69.1 %all-to-all-done.3 = f32[2,128,1,96,48]{3,4,2,0,1:T(8,128)} async-done(((f32[2,128,1,96,48]{3,4,2,0,1:T(8,128)}), f32[2,128,1,96,48]{3,4,2,0,1:T(8,128)}, u32[]{:S(2)}, u32[]{:S(2)}) %all-to-all-start.3) | async-done | bytes 4718624 | tf_op jit(solution)/shard_map/all_to_all | solution.py:96
  374.1 6.2 %copy.94 = f32[2,128,1,96,48]{1,4,3,0,2:T(8,128)} copy(f32[2,128,1,96,48]{3,4,2,0,1:T(8,128)} %all-to-all-done.3) | data formatting | bytes 9437184 | tf_op jit(solution)/shard_map/all_to_all | solution.py:96
  380.3 2.9 multiply_dynamic-update-slice_fusion.4
  384.8 2.3 multiply_dynamic-update-slice_fusion.3
  391.2 3.6 multiply_dynamic-update-slice_fusion
  394.8 4.4 copy-done.2
  399.2 13.7 %copy.96 = f32[640,4608]{1,0:T(8,128)} copy(f32[640,4608]{0,1:T(8,128)} %bitcast.195) | data formatting | bytes 23592960 | tf_op jit(solution)/shard_map/pc,pd->cd/dot_general | solution.py:146
  413.0 14.1 %multiply_reduce_fusion.1 = (f32[128]{0:T(128)S(1)}, f32[96,48]{1,0:T(8,128)S(1)}, f32[96,48]{1,0:T(8,128)S(1)}, f32[96,48,128]{2,1,0:T(8,128)}) fusion(f32[96,48,128]{2,1,0:T(8,128)S(1)} %copy-done.1, f32[96,48]{1,0:T(8,128)S(1)} %add_rsqrt_fusion.1, f32[96,48]{1,0:T(8,128)S(1)} %broadcast_multiply_fusion.6, f32[128]{0:T(128)S(1)} %get-tuple-element.14, ...), kind=kOutput, calls=%fused_computation.14 | convolution fusion | flops 4534557696 | bytes 16917504 | tf_op jit(solution)/shard_map/dot_general | solution.py:142
  427.1 14.0 %fusion.44 = f32[128,5,128]{2,0,1:T(8,128)S(1)} fusion(f32[4608,128,1]{1,0,2:T(8,128)S(1)} %bitcast.201, f32[5,128,4608]{2,1,0:T(8,128)S(1)} %bitcast.196), kind=kOutput, calls=%fused_computation.82 | convolution fusion | flops 4529848320 | bytes 14483456 | tf_op jit(solution)/shard_map/pc,pd->cd/dot_general | solution.py:146
  441.6 79.5 %all_to_all.39 = f32[16,770,128]{2,1,0:T(8,128)} all-to-all(f32[16,770,128]{2,1,0:T(8,128)S(1)} %broadcast_in_dim.13), channel_id=1, replica_groups=mesh['row'=8,'col'=16] {'col'}, dimensions={0} | all-to-all | bytes 12615680 | tf_op jit(solution)/shard_map/all_to_all | solution.py:12
  521.1 3.1 reduce_sum.118
  526.2 7.0 %all-to-all-start.5 = ((f32[8,770,128]{2,1,0:T(8,128)}), f32[8,770,128]{2,1,0:T(8,128)}, u32[]{:S(2)}, u32[]{:S(2)}) async-start(f32[8,770,128]{2,1,0:T(8,128)} %broadcast_in_dim.14), calls=%async_computation.5 | async-start | bytes 6356992 | tf_op jit(solution)/shard_map/all_to_all | solution.py:12
  533.2 6.1 %subtract_multiply_fusion = f32[96,48,128]{2,1,0:T(8,128)} fusion(f32[96,48,128]{2,1,0:T(8,128)} %get-tuple-element.16, f32[96,48,128]{2,1,0:T(8,128)S(1)} %copy-done.1, f32[96,48]{1,0:T(8,128)S(1)} %broadcast_multiply_fusion.1, f32[96,48]{1,0:T(8,128)S(1)} %broadcast_multiply_fusion.2, f32[128]{0:T(128)S(1)} %get-tuple-element.14, ...), kind=kLoop, calls=%fused_computation.17 | loop fusion | flops 4128768 | bytes 7152128 | tf_op jit(solution)/shard_map/mul | solution.py:30
  539.4 39.4 %all-to-all-done.5 = f32[8,770,128]{2,1,0:T(8,128)} async-done(((f32[8,770,128]{2,1,0:T(8,128)}), f32[8,770,128]{2,1,0:T(8,128)}, u32[]{:S(2)}, u32[]{:S(2)}) %all-to-all-start.5) | async-done | bytes 3153952 | tf_op jit(solution)/shard_map/all_to_all | solution.py:12
  578.7 2.1 reduce_sum.119
  (70 shorter events, 18.7 us)
Async XLA Ops:
  0.6 2.5 copy-start
  0.6 4.0 copy-start.21
  4.7 1.6 copy-start.20
  6.2 8.9 %copy-start.5 = (f32[96,48,128]{2,1,0:T(8,128)}, f32[96,48,128]{2,1,0:T(8,128)S(1)}, u32[]{:S(2)}) copy-start(f32[96,48,128]{2,1,0:T(8,128)S(1)} %fusion.12) | copy-start | bytes 7077892
  8.3 11.8 %copy-start.14 = (f32[96,48,128]{2,1,0:T(8,128)}, f32[96,48,128]{2,1,0:T(8,128)S(1)}, u32[]{:S(2)}) copy-start(f32[96,48,128]{2,1,0:T(8,128)S(1)} %add_divide_fusion.1) | copy-start | bytes 7077892
  122.2 12.6 %copy-start.8 = (f32[1,1,8,96,16,48]{3,5,4,2,0,1:T(8,128)}, f32[1,1,8,96,16,48]{3,5,4,2,0,1:T(8,128)S(1)}, u32[]{:S(2)}) copy-start(f32[1,1,8,96,16,48]{3,5,4,2,0,1:T(8,128)S(1)} %get-tuple-element.10) | copy-start | bytes 7077892
  145.3 7.0 %copy-start.6 = (f32[96,48,128]{2,1,0:T(8,128)S(1)}, f32[96,48,128]{2,1,0:T(8,128)}, u32[]{:S(2)}) copy-start(f32[96,48,128]{2,1,0:T(8,128)} %copy-done.5) | copy-start | bytes 7077892
  145.3 47.8 %all-to-all-start.1 = ((f32[1,128,1,96,48]{3,4,2,0,1:T(8,128)}), f32[1,128,1,96,48]{3,4,2,0,1:T(8,128)}, u32[]{:S(2)}, u32[]{:S(2)}) async-start(f32[1,128,1,96,48]{3,4,2,0,1:T(8,128)} %bitcast.205), calls=%async_computation.1 | async-start | bytes 6291456 | tf_op jit(solution)/shard_map/all_to_all | solution.py:85
  195.7 2.2 copy-start.10
  195.7 2.4 copy-start.12
  210.0 47.0 %all-to-all-start.2 = ((f32[1,128,96,48]{2,3,0,1:T(8,128)}), f32[1,128,96,48]{2,3,0,1:T(8,128)}, u32[]{:S(2)}, u32[]{:S(2)}) async-start(f32[1,128,96,48]{2,3,0,1:T(8,128)} %copy.88), calls=%async_computation.2 | async-start | bytes 6291456 | tf_op jit(solution)/shard_map/all_to_all | solution.py:79
  216.2 5.6 copy-start.9
  267.1 11.0 %copy-start.18 = (f32[768,768]{0,1:T(8,128)S(1)}, f32[768,768]{0,1:T(8,128)}, u32[]{:S(2)}) copy-start(f32[768,768]{0,1:T(8,128)} %reshape.192) | copy-start | bytes 7077892
  267.1 11.0 %copy-start.19 = (f32[768,768]{0,1:T(8,128)S(1)}, f32[768,768]{0,1:T(8,128)}, u32[]{:S(2)}) copy-start(f32[768,768]{0,1:T(8,128)} %reshape.190) | copy-start | bytes 7077892
  290.5 83.5 %all-to-all-start.3 = ((f32[2,128,1,96,48]{3,4,2,0,1:T(8,128)}), f32[2,128,1,96,48]{3,4,2,0,1:T(8,128)}, u32[]{:S(2)}, u32[]{:S(2)}) async-start(f32[2,128,1,96,48]{3,4,2,0,1:T(8,128)} %copy.93), calls=%async_computation.3 | async-start | bytes 12582912 | tf_op jit(solution)/shard_map/all_to_all | solution.py:96
  380.3 3.8 copy-start.4
  380.3 4.5 copy-start.16
  384.8 2.4 copy-start.15
  387.2 1.7 copy-start.17
  388.9 1.7 copy-start.11
  388.9 2.4 copy-start.13
  394.8 4.4 copy-start.2
  399.2 13.7 %copy-start.1 = (f32[96,48,128]{2,1,0:T(8,128)S(1)}, f32[96,48,128]{2,1,0:T(8,128)}, u32[]{:S(2)}) copy-start(f32[96,48,128]{2,1,0:T(8,128)} %param.5) | copy-start | bytes 7077892
  413.0 14.2 %copy-start.3 = (f32[640,4608]{1,0:T(8,128)S(1)}, f32[640,4608]{1,0:T(8,128)}, u32[]{:S(2)}) copy-start(f32[640,4608]{1,0:T(8,128)} %copy.96) | copy-start | bytes 35389444
  413.0 14.2 %copy-start.7 = (f32[96,48,128]{2,1,0:T(8,128)S(1)}, f32[96,48,128]{2,1,0:T(8,128)}, u32[]{:S(2)}) copy-start(f32[96,48,128]{2,1,0:T(8,128)} %copy-done.5) | copy-start | bytes 7077892
  526.2 52.5 %all-to-all-start.5 = ((f32[8,770,128]{2,1,0:T(8,128)}), f32[8,770,128]{2,1,0:T(8,128)}, u32[]{:S(2)}, u32[]{:S(2)}) async-start(f32[8,770,128]{2,1,0:T(8,128)} %broadcast_in_dim.14), calls=%async_computation.5 | async-start | bytes 6356992 | tf_op jit(solution)/shard_map/all_to_all | solution.py:12
where the time goes:
time: 593 us; the launch traced here: 582 us
  waiting for transfers between devices  168 us (28%)
  blocking collectives  166 us (28%)
  local copies, waits for them, and re-layouts  94.4 us (16%)
  matrix products  89.8 us (15%)
  other arithmetic  36.7 us (6%)
  starting transfers between devices  25.9 us (4%)
    all_to_all x1, blocking collectives, acts_to_channels(): lax.all_to_all(stacked, ('row', 'col'), split_axis=1, concat_axis=2, tile...  86.9 us
    all_to_all x1, blocking collectives, from_everyone(): return lax.all_to_all(copies, axis, split_axis=0, concat_axis=0, tiled=True)  79.5 us
    all_to_all x1, waiting for transfers between devices, grads_to_positions(): lax.all_to_all(split_direct(chan_stack, tile_rows, tile_cols), ('row', 'c...  69.1 us
    all_to_all x1, waiting for transfers between devices, from_everyone(): return lax.all_to_all(copies, axis, split_axis=0, concat_axis=0, tiled=True)  39.4 us
    all_to_all x1, waiting for transfers between devices, tri_to_positions(): lax.all_to_all(split_direct(chan_stack, tile_rows, tile_cols), ('row', 'c...  36.5 us
    dot_general x7, matrix products, project(): return jnp.einsum('ijc,cd->ijd', operand, weight, precision=highest)  24.3 us
    all_to_all x1, waiting for transfers between devices, dtri_to_channels(): lax.all_to_all(stacked, ('row', 'col'), split_axis=1, concat_axis=2, tile...  23 us
    slice x3, local copies, waits for them, and re-layouts, on_device(): chan_acts[1]  14.5 us
  transfers between devices with their start and end apart: 4, of which 4 were waited for; matrix products, arithmetic and copies ran while one was open for 6% of the time, Pallas kernels for 0%

commit v1 on v0

v1 whole, which is shorter than its diff:
```python
import functools

import jax
import jax.numpy as jnp
from jax import lax
from jax.experimental import pallas as pl
from jax.experimental.pallas import tpu as pltpu
from jax.sharding import PartitionSpec as P

EPS = 1e-05
F32 = jnp.float32
BF16 = jnp.bfloat16
MESH = pl.DeviceIdType.MESH
VLIM = 60 * 2**20


def params(**kw):
    return pltpu.CompilerParams(vmem_limit_bytes=VLIM, **kw)


def split(v):
    hi = v.astype(BF16)
    lo = (v - hi.astype(F32)).astype(BF16)
    return hi, lo


def dot3(lhs, rhs, dims):
    (lh, ll), (rh, rl) = lhs, rhs
    d = functools.partial(
        lax.dot_general, dimension_numbers=(dims, ((), ())), preferred_element_type=F32
    )
    return d(lh, rh) + (d(lh, rl) + d(ll, rh))


NN = ((1,), (0,))
NT = ((1,), (1,))
TN = ((0,), (0,))


def place():
    row = lax.axis_index("row")
    col = lax.axis_index("col")
    return row // 2, col // 4, lax.rem(row, 2) * 2 + lax.rem(col // 2, 2), lax.rem(col, 2)


def partner(spot, step):
    x, y, z, core = spot
    a, b, c, d = step
    x = lax.rem(x + a, 4)
    y = lax.rem(y + b, 4)
    z = lax.rem(z + c, 4)
    core = lax.rem(core + d, 2)
    return x * 2 + z // 2, y * 4 + lax.rem(z, 2) * 2 + core


def steps():
    out = []
    for s in range(1, 128):
        o = (s * 45) % 128
        out.append((o // 2 % 4, o // 8 % 4, o // 32, o % 2))
    return out


def exchange_kernel(count, *refs):
    srcs = refs[:count]
    dsts = refs[count : 2 * count]
    send_sem, recv_sem = refs[2 * count :]
    spot = place()
    me = lax.axis_index("row") * 16 + lax.axis_index("col")
    barrier = pltpu.get_barrier_semaphore()
    for step in steps():
        r, q = partner(spot, step)
        pl.semaphore_signal(
            barrier, inc=1, device_id={"row": r, "col": q}, device_id_type=MESH
        )
    pl.semaphore_wait(barrier, 127)
    for n in range(count):
        own = pltpu.make_async_copy(
            srcs[n].at[pl.ds(me, 1), :], dsts[n].at[pl.ds(me, 1), :], recv_sem.at[n]
        )
        own.start()
        for step in steps():
            r, q = partner(spot, step)
            to = r * 16 + q
            pltpu.make_async_remote_copy(
                src_ref=srcs[n].at[pl.ds(to, 1), :],
                dst_ref=dsts[n].at[pl.ds(me, 1), :],
                send_sem=send_sem.at[n],
                recv_sem=recv_sem.at[n],
                device_id={"row": r, "col": q},
                device_id_type=MESH,
            ).start()
    for n in range(count):
        pltpu.make_async_copy(srcs[n], dsts[n], recv_sem.at[n]).wait()
        pltpu.make_async_copy(
            srcs[n].at[pl.ds(0, 120), :], dsts[n].at[pl.ds(0, 120), :], send_sem.at[n]
        ).wait()
        for row in range(120, 127):
            pltpu.make_async_copy(
                srcs[n].at[pl.ds(row, 1), :], dsts[n].at[pl.ds(row, 1), :], send_sem.at[n]
            ).wait()


def exchange(ident, *arrays):
    count = len(arrays)
    return pl.pallas_call(
        functools.partial(exchange_kernel, count),
        out_shape=[jax.ShapeDtypeStruct(a.shape, a.dtype) for a in arrays],
        in_specs=[pl.BlockSpec(memory_space=pl.ANY)] * count,
        out_specs=[pl.BlockSpec(memory_space=pl.ANY)] * count,
        scratch_shapes=[pltpu.SemaphoreType.DMA((count,))] * 2,
        compiler_params=params(collective_id=ident, has_side_effects=True),
        name=f"exchange_{ident}",
    )(*arrays)


def sum_kernel(x_ref, out_ref, parts, mine, send_a, recv_a, send_b, recv_b):
    spot = place()
    me = lax.axis_index("row") * 16 + lax.axis_index("col")
    barrier = pltpu.get_barrier_semaphore()
    for step in steps():
        r, q = partner(spot, step)
        pl.semaphore_signal(
            barrier, inc=1, device_id={"row": r, "col": q}, device_id_type=MESH
        )
    pl.semaphore_wait(barrier, 127)

    def rows_of(owner):
        return pl.ds(pl.multiple_of(owner * 8, 8), 8)

    for step in steps():
        r, q = partner(spot, step)
        to = r * 16 + q
        pltpu.make_async_remote_copy(
            src_ref=x_ref.at[rows_of(to), :],
            dst_ref=parts.at[rows_of(me), :],
            send_sem=send_a,
            recv_sem=recv_a,
            device_id={"row": r, "col": q},
            device_id_type=MESH,
        ).start()
    pltpu.make_async_copy(x_ref.at[rows_of(me), :], parts.at[rows_of(me), :], recv_a).start()
    pltpu.make_async_copy(x_ref, parts, recv_a).wait()
    total = parts[...].reshape(128, 8, 128).sum(0)
    mine[...] = total
    for step in steps():
        r, q = partner(spot, step)
        pltpu.make_async_remote_copy(
            src_ref=mine,
            dst_ref=out_ref.at[rows_of(me), :],
            send_sem=send_b,
            recv_sem=recv_b,
            device_id={"row": r, "col": q},
            device_id_type=MESH,
        ).start()
    pltpu.make_async_copy(mine, out_ref.at[rows_of(me), :], recv_b).start()
    pltpu.make_async_copy(x_ref, out_ref, recv_b).wait()
    some = x_ref.at[pl.ds(0, 127 * 8), :]
    into = parts.at[pl.ds(0, 127 * 8), :]
    pltpu.make_async_copy(some, into, send_a).wait()
    pltpu.make_async_copy(some, into, send_b).wait()


def sum_everywhere(ident, x):
    return pl.pallas_call(
        sum_kernel,
        out_shape=jax.ShapeDtypeStruct(x.shape, x.dtype),
        in_specs=[pl.BlockSpec(memory_space=pl.ANY)],
        out_specs=pl.BlockSpec(memory_space=pl.ANY),
        scratch_shapes=[pltpu.VMEM((1024, 128), F32), pltpu.VMEM((8, 128), F32)]
        + [pltpu.SemaphoreType.DMA] * 4,
        compiler_params=params(collective_id=ident, has_side_effects=True),
        name="sum_everywhere",
    )(x)


def turn_in(ref):
    rows = ref.shape[0]
    flat = ref.reshape(rows * 8, 128)
    parts = [flat[pl.ds(j, rows, stride=8), :] for j in range(8)]
    return jnp.concatenate(parts, axis=0).T


def norm_parts(v):
    scale = 1.0 / v.shape[0]
    mu = jnp.sum(v, axis=0, keepdims=True) * scale
    cen = v - mu
    inv = lax.rsqrt(jnp.sum(cen * cen, axis=0, keepdims=True) * scale + EPS)
    return cen * inv, inv


def norm_back(h, hat, inv):
    scale = 1.0 / h.shape[0]
    m1 = jnp.sum(h, axis=0, keepdims=True) * scale
    m2 = jnp.sum(h * hat, axis=0, keepdims=True) * scale
    return inv * (h - m1 - hat * m2)


def sigmoid(v):
    return 1.0 / (1.0 + jnp.exp(-v))


def front_kernel(x_ref, mask_ref, gain_ref, wh_ref, wl_ref, *outs):
    a_ref, b_ref, hat_ref, inv_ref, la_ref, sa_ref, lb_ref, sb_ref, sg_ref = outs
    hat, inv = norm_parts(turn_in(x_ref))
    hat_ref[...] = hat
    inv_ref[...] = inv
    normed = split(hat * gain_ref[:, 0:1])
    mask = mask_ref[...]

    def proj(n):
        rows = pl.ds(n * 128, 128)
        return dot3((wh_ref[rows, :], wl_ref[rows, :]), normed, NN)

    lin = proj(0)
    sig = sigmoid(proj(1))
    la_ref[...] = lin
    sa_ref[...] = sig
    a_ref[...] = mask * sig * lin
    lin = proj(2)
    sig = sigmoid(proj(3))
    lb_ref[...] = lin
    sb_ref[...] = sig
    b_ref[...] = mask * sig * lin
    sg_ref[...] = sigmoid(proj(4))


def middle_kernel(t_ref, go_ref, sg_ref, gain_ref, wh_ref, wl_ref, uh_ref, ul_ref, *outs):
    dt_ref, dg_ref, ow_ref, gt_ref = outs
    tri_hat, tri_inv = norm_parts(t_ref[...])
    gain = gain_ref[:, 1:2]
    tri_norm = split(tri_hat * gain)
    lin_o = dot3((wh_ref[...], wl_ref[...]), tri_norm, NN)
    sig = sg_ref[...]
    d_out = turn_in(go_ref) * sig
    dg_ref[...] = d_out * lin_o * (1.0 - sig)
    d_out = split(d_out)
    d_norm = dot3((uh_ref[...], ul_ref[...]), d_out, NN)
    dt_ref[...] = norm_back(d_norm * gain, tri_hat, tri_inv)

    @pl.when(pl.program_id(0) == 0)
    def _():
        ow_ref[...] = jnp.zeros_like(ow_ref)
        gt_ref[...] = jnp.zeros_like(gt_ref)

    ow_ref[...] += dot3(tri_norm, d_out, NT)
    prod = d_norm * tri_hat
    gt_ref[...] += sum(prod[:, 128 * t : 128 * t + 128] for t in range(6))


def back_kernel(
    da_ref, db_ref, mask_ref, hat_ref, inv_ref, la_ref, sa_ref, lb_ref, sb_ref, dg_ref,
    gain_ref, uh_ref, ul_ref, gp_ref, gw_ref, go_ref,
):
    mask = mask_ref[...]
    hat = hat_ref[...]
    gain = gain_ref[:, 0:1]
    normed = split(hat * gain)

    @pl.when(pl.program_id(0) == 0)
    def _():
        gw_ref[...] = jnp.zeros_like(gw_ref)
        go_ref[...] = jnp.zeros_like(go_ref)

    total = None

    def use(n, grad):
        nonlocal total
        grad = split(grad)
        gw_ref[pl.ds(n * 128, 128), :] += dot3(normed, grad, NT)
        rows = pl.ds(n * 128, 128)
        term = dot3((uh_ref[rows, :], ul_ref[rows, :]), grad, NN)
        total = term if total is None else total + term

    for n, d_ref, l_ref, s_ref in ((0, da_ref, la_ref, sa_ref), (2, db_ref, lb_ref, sb_ref)):
        sig = s_ref[...]
        d_lin = d_ref[...] * mask * sig
        use(n, d_lin)
        use(n + 1, d_lin * l_ref[...] * (1.0 - sig))
    use(4, dg_ref[...])
    prod = total * hat
    go_ref[...] += sum(prod[:, 128 * t : 128 * t + 128] for t in range(6))
    grad = norm_back(total * gain, hat, inv_ref[...]).T
    rows = gp_ref.shape[0]
    flat = gp_ref.reshape(rows * 8, 128)
    for j in range(8):
        flat[pl.ds(j, rows, stride=8), :] = grad[j * rows : (j + 1) * rows, :]


CHUNK = 768
STEPS = 6


def chunked(rows=128):
    return pl.BlockSpec((rows, CHUNK), lambda s: (0, s))


def whole(*shape):
    return pl.BlockSpec(shape, lambda s: (0,) * len(shape))


TILE_SPEC = pl.BlockSpec((96, None, 8, 128), lambda s: (0, s, 0, 0))
FULL = jax.ShapeDtypeStruct((128, 4608), F32)


def front(pair4, mask, gains_t, wh, wl):
    return pl.pallas_call(
        front_kernel,
        grid=(STEPS,),
        in_specs=[TILE_SPEC, chunked(1), whole(128, 2), whole(640, 128), whole(640, 128)],
        out_specs=[chunked()] * 3 + [chunked(1)] + [chunked()] * 5,
        out_shape=[FULL] * 3 + [jax.ShapeDtypeStruct((1, 4608), F32)] + [FULL] * 5,
        compiler_params=params(),
        name="front",
    )(pair4, mask, gains_t, wh, wl)


def middle(tri, go4, sig_g, gains_t, wh, wl, uh, ul):
    return pl.pallas_call(
        middle_kernel,
        grid=(STEPS,),
        in_specs=[chunked(), TILE_SPEC, chunked(), whole(128, 2)] + [whole(128, 128)] * 4,
        out_specs=[chunked(), chunked(), whole(128, 128), whole(128, 128)],
        out_shape=[FULL, FULL] + [jax.ShapeDtypeStruct((128, 128), F32)] * 2,
        compiler_params=params(),
        name="middle",
    )(tri, go4, sig_g, gains_t, wh, wl, uh, ul)


def back(da, db, mask, hat, inv, la, sa, lb, sb, dg, gains_t, uh, ul):
    return pl.pallas_call(
        back_kernel,
        grid=(STEPS,),
        in_specs=[chunked(), chunked(), chunked(1), chunked(), chunked(1)]
        + [chunked()] * 5
        + [whole(128, 2), whole(640, 128), whole(640, 128)],
        out_specs=[TILE_SPEC, whole(640, 128), whole(128, 128)],
        out_shape=[
            jax.ShapeDtypeStruct((96, 6, 8, 128), F32),
            jax.ShapeDtypeStruct((640, 128), F32),
            jax.ShapeDtypeStruct((128, 128), F32),
        ],
        compiler_params=params(),
        name="back",
    )(da, db, mask, hat, inv, la, sa, lb, sb, dg, gains_t, uh, ul)


def swap_four(blocks):
    lane = lax.broadcasted_iota(jnp.int32, blocks[0].shape, 1)
    outs = []
    for a in range(4):
        out = None
        for b in range(4):
            shift = (96 * (b - a)) % 384
            moved = blocks[b] if shift == 0 else pltpu.roll(blocks[b], shift, 1)
            out = moved if out is None else jnp.where(lane < 96 * b, out, moved)
        outs.append(out)
    return outs


def read_group(ref, group, half):
    lanes = pl.ds(pl.multiple_of(group * 384, 384), 384)
    return [ref[pl.ds((half * 4 + r) * 16, 16), lanes] for r in range(4)]


def write_group(ref, group, half, blocks):
    lanes = pl.ds(pl.multiple_of(group * 384, 384), 384)
    for r in range(4):
        ref[pl.ds((half * 4 + r) * 16, 16), lanes] = blocks[r]


def gather_matrix(src_ref, hi_ref, lo_ref):
    @pl.loop(0, 12)
    def _(group):
        for half in range(2):
            for k, block in enumerate(swap_four(read_group(src_ref, group, half))):
                hi, lo = split(block)
                rows = pl.ds(pl.multiple_of(group * 64 + k * 16, 16), 16)
                lanes = pl.ds(half * 384, 384)
                hi_ref[rows, lanes] = hi
                lo_ref[rows, lanes] = lo


PITCH = 56


def triangle_kernel(ra_ref, rb_ref, ah_ref, al_ref, bh_ref, bl_ref, out_ref, scr):
    gather_matrix(ra_ref, ah_ref, al_ref)
    gather_matrix(rb_ref, bh_ref, bl_ref)

    @pl.loop(0, 3)
    def _(n):
        lanes = pl.ds(pl.multiple_of(n * 256, 256), 256)
        res = dot3((bh_ref[...], bl_ref[...]), (ah_ref[:, lanes], al_ref[:, lanes]), TN)
        for t in range(2):
            for q in range(16):
                scr[n * 2 + t, pl.ds(q * PITCH, 48), :] = res[
                    q * 48 : q * 48 + 48, t * 128 : t * 128 + 128
                ]

    @pl.loop(0, 12)
    def _(group):
        for half in range(2):
            blocks = []
            for k in range(4):
                parts = [
                    scr.at[half * 3 + t][pl.ds(group * 4 + k, 16, stride=PITCH), :]
                    for t in range(3)
                ]
                blocks.append(jnp.concatenate(parts, axis=1))
            write_group(out_ref, group, half, swap_four(blocks))


def triangle(ra, rb):
    mat = jax.ShapeDtypeStruct((768, 768), BF16)
    return pl.pallas_call(
        triangle_kernel,
        out_shape=[mat] * 4 + [FULL],
        in_specs=[pl.BlockSpec(memory_space=pltpu.VMEM)] * 2,
        out_specs=[pl.BlockSpec(memory_space=pltpu.VMEM)] * 5,
        scratch_shapes=[pltpu.VMEM((6, 16 * PITCH, 128), F32)],
        compiler_params=params(),
        name="triangle",
    )(ra, rb)


def grads_kernel(rd_ref, ah_ref, al_ref, bh_ref, bl_ref, oa_ref, ob_ref, scr, dh, dl, res):
    @pl.loop(0, 12)
    def _(group):
        for half in range(2):
            for k, block in enumerate(swap_four(read_group(rd_ref, group, half))):
                for t in range(3):
                    scr.at[half * 3 + t][pl.ds(group * 4 + k, 16, stride=PITCH), :] = block[
                        :, t * 128 : t * 128 + 128
                    ]

    @pl.loop(0, 16)
    def _(q):
        for t in range(6):
            hi, lo = split(scr[t, pl.ds(pl.multiple_of(q * PITCH, 8), 48), :])
            rows = pl.ds(pl.multiple_of(q * 48, 16), 48)
            dh[rows, pl.ds(t * 128, 128)] = hi
            dl[rows, pl.ds(t * 128, 128)] = lo

    def spread(out_ref):
        @pl.loop(0, 12)
        def _(group):
            for half in range(2):
                blocks = [
                    res[
                        pl.ds(pl.multiple_of(group * 64 + k * 16, 16), 16),
                        pl.ds(half * 384, 384),
                    ]
                    for k in range(4)
                ]
                write_group(out_ref, group, half, swap_four(blocks))

    @pl.loop(0, 3)
    def _(n):
        lanes = pl.ds(pl.multiple_of(n * 256, 256), 256)
        res[:, lanes] = dot3((bh_ref[...], bl_ref[...]), (dh[:, lanes], dl[:, lanes]), NN)

    spread(oa_ref)

    @pl.loop(0, 3)
    def _(n):
        lanes = pl.ds(pl.multiple_of(n * 256, 256), 256)
        res[:, lanes] = dot3((ah_ref[...], al_ref[...]), (dh[lanes, :], dl[lanes, :]), NT)

    spread(ob_ref)


def act_grads(rd, ah, al, bh, bl):
    return pl.pallas_call(
        grads_kernel,
        out_shape=[FULL] * 2,
        in_specs=[pl.BlockSpec(memory_space=pltpu.VMEM)] * 5,
        out_specs=[pl.BlockSpec(memory_space=pltpu.VMEM)] * 2,
        scratch_shapes=[
            pltpu.VMEM((6, 16 * PITCH, 128), F32),
            pltpu.VMEM((768, 768), BF16),
            pltpu.VMEM((768, 768), BF16),
            pltpu.VMEM((768, 768), F32),
        ],
        compiler_params=params(),
        name="act_grads",
    )(rd, ah, al, bh, bl)


def round_split(v):
    hi = lax.reduce_precision(v, 8, 7)
    return hi.astype(BF16), (v - hi).astype(BF16)


def on_device(pair_act, grad_out, residue_mask, norm_gains, weights):
    tile_rows, tile_cols, channels = pair_act.shape
    residues = residue_mask.shape[0]
    row_mask = lax.dynamic_slice_in_dim(
        residue_mask, lax.axis_index("row") * tile_rows, tile_rows
    )
    col_mask = lax.dynamic_slice_in_dim(
        residue_mask, lax.axis_index("col") * tile_cols, tile_cols
    )
    mask = (col_mask[:, None] * row_mask[None, :]).astype(F32).reshape(1, -1)
    gains_t = norm_gains.T
    turned = jnp.transpose(weights, (0, 2, 1))
    wh, wl = round_split(turned.reshape(6 * channels, channels))
    uh, ul = round_split(weights.reshape(6 * channels, channels))
    cut = 5 * channels
    pair4 = pair_act.reshape(tile_rows, tile_cols // 8, 8, channels)
    go4 = grad_out.reshape(tile_rows, tile_cols // 8, 8, channels)
    a, b, hat, inv, la, sa, lb, sb, sg = front(pair4, mask, gains_t, wh[:cut], wl[:cut])
    ra, rb = exchange(0, a, b)
    ah, al, bh, bl, tri = triangle(ra, rb)
    (rt,) = exchange(1, tri)
    dt, dg, out_part, gain_two = middle(
        rt, go4, sg, gains_t, wh[cut:], wl[cut:], uh[cut:], ul[cut:]
    )
    (rd,) = exchange(2, dt)
    oa, ob = act_grads(rd, ah, al, bh, bl)
    da, db = exchange(3, oa, ob)
    grad_pair, weight_part, gain_one = back(
        da, db, mask, hat, inv, la, sa, lb, sb, dg, gains_t, uh[:cut], ul[:cut]
    )
    gains = jnp.stack([gain_one, gain_two]).sum(-1)
    spare = jnp.zeros((1024 - 6 * channels - 2, channels), F32)
    combined = jnp.concatenate([weight_part, out_part, gains, spare], axis=0)
    total = sum_everywhere(4, combined) / residues
    return (
        grad_pair.reshape(pair_act.shape),
        total[: 6 * channels].reshape(6, channels, channels),
        total[6 * channels : 6 * channels + 2],
    )


def solution(mesh):
    return jax.shard_map(
        on_device,
        mesh=mesh,
        in_specs=(P("row", "col", None), P("row", "col", None), P(), P(), P()),
        out_specs=(P("row", "col", None), P(), P()),
        check_vma=False,
    )
```

time: 593 us -> 311 us (0.52); the launches traced: 582 us -> 310 us
  Pallas kernels: 0 us -> 294 us
  waiting for transfers between devices: 168 us -> 0 us
  blocking collectives: 166 us -> 0 us
  matrix products: 89.8 us -> 0 us
  local copies, waits for them, and re-layouts: 94.4 us -> 11.4 us
  other arithmetic: 36.7 us -> 4.21 us
  starting transfers between devices: 25.9 us -> 0 us
    pallas_call x0 -> x10, Pallas kernels: none -> 294 us  [the longest x4 198 us: exchange(): pl.pallas_call(functools.partial(exchange_kernel, count), out_shape=[jax....]
    all_to_all x4 -> x0, waiting for transfers between devices: 168 us -> none  [the longest x1 69.1 us: grads_to_positions(): lax.all_to_all(split_direct(chan_stack, tile_rows, tile_cols), ('row', 'c...]
    all_to_all x2 -> x0, blocking collectives: 166 us -> none  [the longest x1 86.9 us: acts_to_channels(): lax.all_to_all(stacked, ('row', 'col'), split_axis=1, concat_axis=2, tile...]
    dot_general x13 -> x0, matrix products: 89.8 us -> none  [the longest x7 24.3 us: project(): return jnp.einsum('ijc,cd->ijd', operand, weight, precision=highest)]
    all_to_all x4 -> x0, starting transfers between devices: 25.9 us -> none  [the longest x1 7.03 us: from_everyone(): return lax.all_to_all(copies, axis, split_axis=0, concat_axis=0, tiled=True)]
    dot_general x2 -> x0, local copies, waits for them, and re-layouts: 19.8 us -> none  [the longest x1 13.7 us: on_device(): jnp.einsum('pc,pd->cd', flat_normed, grads_cat, precision=highest)]
    transpose x5 -> x1, local copies, waits for them, and re-layouts: 16.4 us -> 1.16 us  [on_device(): turned = jnp.transpose(weights, (0, 2, 1))]
    another operation x3 -> x0, local copies, waits for them, and re-layouts: 13.4 us -> none
  transfers between devices with their start and end apart: 4 -> 0, of which waited for: 4 -> 0; matrix products, arithmetic and copies ran while one was open for 6% -> 0% of each run, Pallas kernels for 0% -> 0%
where the time goes in v1:
time: 311 us; the launch traced here: 310 us
  Pallas kernels  294 us (95%)
  local copies, waits for them, and re-layouts  11.4 us (4%)
  other arithmetic  4.21 us (1%)
    pallas_call x4, Pallas kernels, exchange(): pl.pallas_call(functools.partial(exchange_kernel, count), out_shape=[jax....  198 us
    pallas_call x1, Pallas kernels, sum_everywhere(): pl.pallas_call(sum_kernel, out_shape=jax.ShapeDtypeStruct(x.shape, x.dtyp...  25.2 us
    pallas_call x1, Pallas kernels, act_grads(): pl.pallas_call(grads_kernel, out_shape=[FULL] * 2, in_specs=[pl.BlockSpec...  19.4 us
    pallas_call x1, Pallas kernels, back(): pl.pallas_call(back_kernel, grid=(STEPS,), in_specs=[chunked(), chunked()...  15.9 us
    pallas_call x1, Pallas kernels, triangle(): pl.pallas_call(triangle_kernel, out_shape=[mat] * 4 + [FULL], in_specs=[p...  15.7 us
    pallas_call x1, Pallas kernels, front(): pl.pallas_call(front_kernel, grid=(STEPS,), in_specs=[TILE_SPEC, chunked(...  10.2 us
    pallas_call x1, Pallas kernels, middle(): pl.pallas_call(middle_kernel, grid=(STEPS,), in_specs=[chunked(), TILE_SP...  9.25 us

profile of v1, /device:TPU:1, one launch (start us, length us, event | category | flops | bytes accessed | tf_op | source)
XLA Modules:
  0.0 310.1 jit_solution(4861987604961967679)
XLA Ops:
  0.6 0.0 copy-start
  0.6 0.8 dynamic_slice.7
  1.5 0.8 dynamic_slice.6
  2.2 0.1 pad.3.clone
  2.3 0.1 multiply_convert_fusion
  2.4 0.7 convert_element_type.26.mask_ref
  3.1 1.4 copy.8
  4.5 1.2 copy.9
  5.6 0.1 fusion
  5.7 0.6 slice.43.wl_ref
  6.3 0.7 slice.41.wl_ref
  7.0 0.6 slice.42.wh_ref
  7.6 0.7 slice.40.wh_ref
  8.3 0.0 copy-done
  8.3 0.1 fusion.1
  8.4 0.6 slice.45.ul_ref
  9.0 0.7 slice.47.ul_ref
  9.6 0.6 slice.44.uh_ref
  10.2 0.7 slice.46.uh_ref
  10.9 10.2 %front.1 = (f32[128,4608]{1,0:T(8,128)}, f32[128,4608]{1,0:T(8,128)}, f32[128,4608]{1,0:T(8,128)}, f32[1,4608]{1,0:T(1,128)}, f32[128,4608]{1,0:T(8,128)}, /*ind...) custom-call(f32[96,6,8,128]{3,2,1,0:T(8,128)} %bitcast.15, ...), custom_call_target="tpu_custom_call" | custom-call | tf_op jit(solution)/shard_map/front/pallas_call | solution.py:307
  21.1 65.2 %exchange_0.1 = (f32[128,4608]{1,0:T(8,128)}, f32[128,4608]{1,0:T(8,128)}) custom-call(f32[128,4608]{1,0:T(8,128)} %get-tuple-element.30.refs_0_, f32[128,4608]{1,0:T(8,128)} %get-tuple-element.31.refs_1_), custom_call_target="tpu_custom_call" | custom-call | tf_op jit(solution)/shard_map/exchange_0/pallas_call | solution.py:106
  86.3 15.7 %triangle.1 = (bf16[768,768]{1,0:T(8,128)(2,1)}, bf16[768,768]{1,0:T(8,128)(2,1)}, bf16[768,768]{1,0:T(8,128)(2,1)}, bf16[768,768]{1,0:T(8,128)(2,1)}, f32[128,4608]{1,0:T(8,128)}) custom-call(f32[128,4608]{1,0:T(8,128)} %get-tuple-element.32.ra_ref, f32[128,4608]{1,0:T(8,128)} %get-tuple-element.33.rb_ref), custom_call_target="tpu_custom_call" | custom-call | tf_op jit(solution)/shard_map/triangle/pallas_call | solution.py:416
  102.0 36.2 %exchange_1.1.t_ref = f32[128,4608]{1,0:T(8,128)} custom-call(f32[128,4608]{1,0:T(8,128)} %get-tuple-element.34.refs_0_), custom_call_target="tpu_custom_call" | custom-call | tf_op jit(solution)/shard_map/exchange_1/pallas_call | solution.py:106
  138.3 9.2 %middle.1 = (f32[128,4608]{1,0:T(8,128)}, f32[128,4608]{1,0:T(8,128)}, f32[128,128]{1,0:T(8,128)}, f32[128,128]{1,0:T(8,128)}) custom-call(f32[128,4608]{1,0:T(8,128)} %exchange_1.1.t_ref, f32[96,6,8,128]{3,2,1,0:T(8,128)} %bitcast.14, f32[128,4608]{1,0:T(8,128)} %get-tuple-element.35.sg_ref, f32[128,2]{1,0:T(8,128)} %bitcast.18, ...), custom_call_target="tpu_custom_call" | custom-call | tf_op jit(solution)/shard_map/middle/pallas_call | solution.py:319
  147.5 35.8 %exchange_2.1.rd_ref = f32[128,4608]{1,0:T(8,128)} custom-call(f32[128,4608]{1,0:T(8,128)} %get-tuple-element.36.refs_0_), custom_call_target="tpu_custom_call" | custom-call | tf_op jit(solution)/shard_map/exchange_2/pallas_call | solution.py:106
  183.4 19.4 %act_grads.1 = (f32[128,4608]{1,0:T(8,128)}, f32[128,4608]{1,0:T(8,128)}) custom-call(f32[128,4608]{1,0:T(8,128)} %exchange_2.1.rd_ref, bf16[768,768]{1,0:T(8,128)(2,1)} %get-tuple-element.37.ah_ref, bf16[768,768]{1,0:T(8,128)(2,1)} %get-tuple-element.38.al_ref, bf16[768,768]{1,0:T(8,128)(2,1)} %get-tuple-element.39.bh_ref, ...), custom_call_target="tpu_custom_call" | custom-call | tf_op jit(solution)/shard_map/act_grads/pallas_call | solution.py:474
  202.7 60.9 %exchange_3.1 = (f32[128,4608]{1,0:T(8,128)}, f32[128,4608]{1,0:T(8,128)}) custom-call(f32[128,4608]{1,0:T(8,128)} %get-tuple-element.41.refs_0_, f32[128,4608]{1,0:T(8,128)} %get-tuple-element.42.refs_1_), custom_call_target="tpu_custom_call" | custom-call | tf_op jit(solution)/shard_map/exchange_3/pallas_call | solution.py:106
  263.7 0.0 copy-start.2
  263.7 0.0 copy-start.1
  263.7 15.9 %back.1 = (f32[96,6,8,128]{3,2,1,0:T(8,128)}, f32[640,128]{1,0:T(8,128)}, f32[128,128]{1,0:T(8,128)}) custom-call(f32[128,4608]{1,0:T(8,128)} %get-tuple-element.43.da_ref, f32[128,4608]{1,0:T(8,128)} %get-tuple-element.44.db_ref, f32[1,4608]{1,0:T(1,128)} %convert_element_type.26.mask_ref, f32[128,4608]{1,0:T(8,128)} %get-tuple-element.45.hat_ref, ...), custom_call_target="tpu_custom_call" | custom-call | tf_op jit(solution)/shard_map/back/pallas_call | solution.py:331
  279.5 0.0 copy-done.2
  279.6 0.9 maximum_reduce_fusion
  280.5 0.0 copy-done.1
  280.5 2.0 maximum_maximum_fusion.x_ref
  282.5 25.2 %sum_everywhere.1 = f32[1024,128]{1,0:T(8,128)} custom-call(f32[1024,128]{1,0:T(8,128)} %maximum_maximum_fusion.x_ref), custom_call_target="tpu_custom_call" | custom-call | tf_op jit(solution)/shard_map/sum_everywhere/pallas_call | solution.py:165
  307.7 1.1 broadcast_multiply_fusion
  308.8 0.6 slice.49
  309.4 0.8 slice.48
  (1 shorter events, 0.0 us)
Async XLA Ops:
  0.6 7.7 %copy-start = (f32[6,128,128]{2,1,0:T(8,128)S(1)}, f32[6,128,128]{2,1,0:T(8,128)}, u32[]{:S(2)}) copy-start(f32[6,128,128]{2,1,0:T(8,128)} %param.9) | copy-start | bytes 1179652
  263.7 15.9 %copy-start.2 = (f32[128,128]{1,0:T(8,128)S(1)}, f32[128,128]{1,0:T(8,128)}, u32[]{:S(2)}) copy-start(f32[128,128]{1,0:T(8,128)} %get-tuple-element.56) | copy-start | bytes 196612
  263.7 16.8 %copy-start.1 = (f32[128,128]{1,0:T(8,128)S(1)}, f32[128,128]{1,0:T(8,128)}, u32[]{:S(2)}) copy-start(f32[128,128]{1,0:T(8,128)} %get-tuple-element.54) | copy-start | bytes 196612

commit v2 on v1

v2 whole, which is shorter than its diff:
```python
import functools

import jax
import jax.numpy as jnp
from jax import lax
from jax.experimental import pallas as pl
from jax.experimental.pallas import tpu as pltpu
from jax.sharding import PartitionSpec as P

EPS = 1e-05
F32 = jnp.float32
BF16 = jnp.bfloat16
MESH = pl.DeviceIdType.MESH
VLIM = 60 * 2**20


def params(**kw):
    return pltpu.CompilerParams(vmem_limit_bytes=VLIM, **kw)


def split(v):
    hi = v.astype(BF16)
    lo = (v - hi.astype(F32)).astype(BF16)
    return hi, lo


def dot3(lhs, rhs, dims):
    (lh, ll), (rh, rl) = lhs, rhs
    d = functools.partial(
        lax.dot_general, dimension_numbers=(dims, ((), ())), preferred_element_type=F32
    )
    return d(lh, rh) + (d(lh, rl) + d(ll, rh))


NN = ((1,), (0,))
NT = ((1,), (1,))
TN = ((0,), (0,))


def place():
    row = lax.axis_index("row")
    col = lax.axis_index("col")
    return row // 2, col // 4, lax.rem(row, 2) * 2 + lax.rem(col // 2, 2), lax.rem(col, 2)


def partner(spot, step):
    x, y, z, core = spot
    a, b, c, d = step
    x = lax.rem(x + a, 4)
    y = lax.rem(y + b, 4)
    z = lax.rem(z + c, 4)
    core = lax.rem(core + d, 2)
    return x * 2 + z // 2, y * 4 + lax.rem(z, 2) * 2 + core


def steps():
    out = []
    for s in range(1, 128):
        o = (s * 45) % 128
        out.append((o // 2 % 4, o // 8 % 4, o // 32, o % 2))
    return out


def row_of(ref, row, lanes):
    return ref.at[pl.ds(row, 1), lanes]


def send_all(src, dst, lanes, send_sem, recv_sem):
    spot = place()
    me = lax.axis_index("row") * 16 + lax.axis_index("col")
    for step in steps():
        r, q = partner(spot, step)
        pltpu.make_async_remote_copy(
            src_ref=row_of(src, r * 16 + q, lanes),
            dst_ref=row_of(dst, me, lanes),
            send_sem=send_sem,
            recv_sem=recv_sem,
            device_id={"row": r, "col": q},
            device_id_type=MESH,
        ).start()
    dst[pl.ds(me, 1), lanes] = src[pl.ds(me, 1), lanes]


def wait_all(tally, part, sem):
    some = tally.at[pl.ds(0, 127 * (part[1] - part[0]))]
    pltpu.make_async_copy(some, some, sem).wait()


def sum_kernel(x_ref, out_ref, parts, mine, send_a, recv_a, send_b, recv_b):
    spot = place()
    me = lax.axis_index("row") * 16 + lax.axis_index("col")
    barrier = pltpu.get_barrier_semaphore()
    for step in steps():
        r, q = partner(spot, step)
        pl.semaphore_signal(
            barrier, inc=1, device_id={"row": r, "col": q}, device_id_type=MESH
        )
    pl.semaphore_wait(barrier, 127)

    def rows_of(owner):
        return pl.ds(pl.multiple_of(owner * 8, 8), 8)

    for step in steps():
        r, q = partner(spot, step)
        to = r * 16 + q
        pltpu.make_async_remote_copy(
            src_ref=x_ref.at[rows_of(to), :],
            dst_ref=parts.at[rows_of(me), :],
            send_sem=send_a,
            recv_sem=recv_a,
            device_id={"row": r, "col": q},
            device_id_type=MESH,
        ).start()
    pltpu.make_async_copy(x_ref.at[rows_of(me), :], parts.at[rows_of(me), :], recv_a).start()
    pltpu.make_async_copy(x_ref, parts, recv_a).wait()
    total = parts[...].reshape(128, 8, 128).sum(0)
    mine[...] = total
    for step in steps():
        r, q = partner(spot, step)
        pltpu.make_async_remote_copy(
            src_ref=mine,
            dst_ref=out_ref.at[rows_of(me), :],
            send_sem=send_b,
            recv_sem=recv_b,
            device_id={"row": r, "col": q},
            device_id_type=MESH,
        ).start()
    pltpu.make_async_copy(mine, out_ref.at[rows_of(me), :], recv_b).start()
    pltpu.make_async_copy(x_ref, out_ref, recv_b).wait()
    some = x_ref.at[pl.ds(0, 127 * 8), :]
    into = parts.at[pl.ds(0, 127 * 8), :]
    pltpu.make_async_copy(some, into, send_a).wait()
    pltpu.make_async_copy(some, into, send_b).wait()


def sum_everywhere(ident, x):
    return pl.pallas_call(
        sum_kernel,
        out_shape=jax.ShapeDtypeStruct(x.shape, x.dtype),
        in_specs=[pl.BlockSpec(memory_space=pl.ANY)],
        out_specs=pl.BlockSpec(memory_space=pl.ANY),
        scratch_shapes=[pltpu.VMEM((1024, 128), F32), pltpu.VMEM((8, 128), F32)]
        + [pltpu.SemaphoreType.DMA] * 4,
        compiler_params=params(collective_id=ident, has_side_effects=True),
        name="sum_everywhere",
    )(x)


def turn_in(ref):
    rows = ref.shape[0]
    flat = ref.reshape(rows * 8, 128)
    parts = [flat[pl.ds(j, rows, stride=8), :] for j in range(8)]
    return jnp.concatenate(parts, axis=0).T


def norm_parts(v):
    scale = 1.0 / v.shape[0]
    mu = jnp.sum(v, axis=0, keepdims=True) * scale
    cen = v - mu
    inv = lax.rsqrt(jnp.sum(cen * cen, axis=0, keepdims=True) * scale + EPS)
    return cen * inv, inv


def norm_back(h, hat, inv):
    scale = 1.0 / h.shape[0]
    m1 = jnp.sum(h, axis=0, keepdims=True) * scale
    m2 = jnp.sum(h * hat, axis=0, keepdims=True) * scale
    return inv * (h - m1 - hat * m2)


def sigmoid(v):
    return 1.0 / (1.0 + jnp.exp(-v))


def swap_four(blocks):
    lane = lax.broadcasted_iota(jnp.int32, blocks[0].shape, 1)
    outs = []
    for a in range(4):
        out = None
        for b in range(4):
            shift = (96 * (b - a)) % 384
            moved = blocks[b] if shift == 0 else pltpu.roll(blocks[b], shift, 1)
            out = moved if out is None else jnp.where(lane < 96 * b, out, moved)
        outs.append(out)
    return outs


def read_group(ref, group, half):
    lanes = pl.ds(pl.multiple_of(group * 384, 384), 384)
    return [ref[pl.ds((half * 4 + r) * 16, 16), lanes] for r in range(4)]


def write_group(ref, group, half, blocks):
    lanes = pl.ds(pl.multiple_of(group * 384, 384), 384)
    for r in range(4):
        ref[pl.ds((half * 4 + r) * 16, 16), lanes] = blocks[r]


PITCH = 56
UNIT = 1536


def lanes_of(part):
    return pl.ds(part[0] * UNIT, (part[1] - part[0]) * UNIT)


def groups_of(part):
    return pl.loop(part[0] * 4, part[1] * 4)


def chunks_of(part):
    return pl.loop(part[0] * 2, part[1] * 2)


def rows_of(part):
    return pl.ds(part[0] * 256, (part[1] - part[0]) * 256)


def gather_matrix(src_ref, hi_ref, lo_ref, part):
    @groups_of(part)
    def _(group):
        for half in range(2):
            for k, block in enumerate(swap_four(read_group(src_ref, group, half))):
                hi, lo = split(block)
                rows = pl.ds(pl.multiple_of(group * 64 + k * 16, 16), 16)
                lanes = pl.ds(half * 384, 384)
                hi_ref[rows, lanes] = hi
                lo_ref[rows, lanes] = lo


def spread_pitched(scr, out_ref, part):
    @groups_of(part)
    def _(group):
        for half in range(2):
            blocks = []
            for k in range(4):
                pieces = [
                    scr.at[half * 3 + t][pl.ds(group * 4 + k, 16, stride=PITCH), :]
                    for t in range(3)
                ]
                blocks.append(jnp.concatenate(pieces, axis=1))
            write_group(out_ref, group, half, swap_four(blocks))


def spread_rows(res, out_ref, part):
    @groups_of(part)
    def _(group):
        for half in range(2):
            blocks = [
                res[
                    pl.ds(pl.multiple_of(group * 64 + k * 16, 16), 16),
                    pl.ds(half * 384, 384),
                ]
                for k in range(4)
            ]
            write_group(out_ref, group, half, swap_four(blocks))


def gather_pitched(src_ref, scr, part):
    @groups_of(part)
    def _(group):
        for half in range(2):
            for k, block in enumerate(swap_four(read_group(src_ref, group, half))):
                for t in range(3):
                    scr.at[half * 3 + t][pl.ds(group * 4 + k, 16, stride=PITCH), :] = block[
                        :, t * 128 : t * 128 + 128
                    ]


A_PARTS = ((0, 2), (2, 3))
T_PARTS = ((0, 2), (2, 3))
D_PARTS = ((0, 2), (2, 3))
DA_PARTS = ((0, 1), (1, 3))
DB_PARTS = ((0, 2), (2, 3))
ALL = (0, 3)
SENDS = 11


def step_kernel(
    pair_hbm, go_hbm, mask_ref, gain_ref, w_ref, gp_hbm, gw_ref, ow_ref, g1_ref, g2_ref,
    xin, gin, s1, s2, r1, r2, r3, hat_ref, inv_ref, nh, nl, la, sa, lb, sb, sg, dg,
    ah, al, bh, bl, dh, dl, res, scr, th, tl, uh, ul, tally,
    in_sem, go_sem, out_sem, send_sem, recv_sem,
):
    spot = place()
    for s in range(6):
        pltpu.make_async_copy(pair_hbm.at[:, s], xin.at[s], in_sem.at[s]).start()
    for s in range(6):
        pltpu.make_async_copy(go_hbm.at[:, s], gin.at[s], go_sem.at[s]).start()
    barrier = pltpu.get_barrier_semaphore()
    for step in steps():
        r, q = partner(spot, step)
        pl.semaphore_signal(
            barrier, inc=1, device_id={"row": r, "col": q}, device_id_type=MESH
        )
    for n in range(6):
        rows = pl.ds(n * 128, 128)
        th[rows, :], tl[rows, :] = split(w_ref[n].T)
        uh[rows, :], ul[rows, :] = split(w_ref[n])
    gw_ref[...] = jnp.zeros_like(gw_ref)
    ow_ref[...] = jnp.zeros_like(ow_ref)
    g1_ref[...] = jnp.zeros_like(g1_ref)
    g2_ref[...] = jnp.zeros_like(g2_ref)
    gain_in = gain_ref[:, 0:1]
    gain_tri = gain_ref[:, 1:2]

    def wide(s):
        return pl.ds(pl.multiple_of(s * 768, 768), 768)

    def weight(n, hi=th, lo=tl):
        rows = pl.ds(n * 128, 128)
        return hi[rows, :], lo[rows, :]

    def side(n, lanes, lin_ref, sig_ref, out_ref):
        normed = (nh[:, lanes], nl[:, lanes])
        lin = dot3(weight(n), normed, NN)
        sig = sigmoid(dot3(weight(n + 1), normed, NN))
        lin_ref[:, lanes] = lin
        sig_ref[:, lanes] = sig
        out_ref[:, lanes] = mask_ref[:, lanes] * sig * lin

    @chunks_of(ALL)
    def _(s):
        lanes = wide(s)
        pltpu.make_async_copy(pair_hbm.at[:, s], xin.at[s], in_sem.at[s]).wait()
        hat, inv = norm_parts(turn_in(xin.at[s]))
        hat_ref[:, lanes] = hat
        inv_ref[:, lanes] = inv
        nh[:, lanes], nl[:, lanes] = split(hat * gain_in)
        side(2, lanes, lb, sb, s2)

    pl.semaphore_wait(barrier, 127)
    which = iter(range(SENDS))

    def send(src, dst, part):
        n = next(which)
        lanes = lanes_of(part)
        send_all(src, dst, lanes, send_sem.at[n], recv_sem.at[n])
        return (
            lambda: wait_all(tally, part, send_sem.at[n]),
            lambda: wait_all(tally, part, recv_sem.at[n]),
        )

    b_out, b_in = send(s2, r2, ALL)
    moves = []
    for part in A_PARTS:

        @chunks_of(part)
        def _(s):
            side(0, wide(s), la, sa, s1)

        moves.append(send(s1, r1, part))

    @chunks_of(ALL)
    def _(s):
        lanes = wide(s)
        sg[:, lanes] = sigmoid(dot3(weight(4), (nh[:, lanes], nl[:, lanes]), NN))

    b_in()
    gather_matrix(r2, bh, bl, ALL)
    for i, part in enumerate(A_PARTS):
        moves[i][1]()
        gather_matrix(r1, ah, al, part)
        rows = rows_of(part)

        @pl.loop(0, 3)
        def _(n):
            lanes = pl.ds(pl.multiple_of(n * 256, 256), 256)
            got = dot3((bh[rows, :], bl[rows, :]), (ah[rows, lanes], al[rows, lanes]), TN)
            if i > 0:
                got = got + res[:, lanes]
            if i < len(A_PARTS) - 1:
                res[:, lanes] = got
            else:
                for t in range(2):
                    for q in range(16):
                        scr[n * 2 + t, pl.ds(q * PITCH, 48), :] = got[
                            q * 48 : q * 48 + 48, t * 128 : t * 128 + 128
                        ]

    for out, _in in moves:
        out()
    moves = []
    for part in T_PARTS:
        spread_pitched(scr, s1, part)
        moves.append(send(s1, r3, part))

    b_out()
    later = []
    for i, part in enumerate(D_PARTS):
        moves[i][1]()

        @chunks_of(part)
        def _(s):
            lanes = wide(s)
            pltpu.make_async_copy(go_hbm.at[:, s], gin.at[s], go_sem.at[s]).wait()
            tri_hat, tri_inv = norm_parts(r3[:, lanes])
            tri_norm = split(tri_hat * gain_tri)
            lin_o = dot3(weight(5), tri_norm, NN)
            sig = sg[:, lanes]
            d_out = turn_in(gin.at[s]) * sig
            dg[:, lanes] = d_out * lin_o * (1.0 - sig)
            d_out = split(d_out)
            d_norm = dot3(weight(5, uh, ul), d_out, NN)
            s2[:, lanes] = norm_back(d_norm * gain_tri, tri_hat, tri_inv)
            ow_ref[...] += dot3(tri_norm, d_out, NT)
            prod = d_norm * tri_hat
            g2_ref[...] += sum(prod[:, 128 * t : 128 * t + 128] for t in range(6))

        later.append(send(s2, r2, part))

    def use(n, lanes, grad):
        grad = split(grad)
        rows = pl.ds(n * 128, 128)
        gw_ref[rows, :] += dot3((nh[:, lanes], nl[:, lanes]), grad, NT)
        return dot3(weight(n, uh, ul), grad, NN)

    @chunks_of(ALL)
    def _(s):
        lanes = wide(s)
        sg[:, lanes] = use(4, lanes, dg[:, lanes])

    for i, part in enumerate(D_PARTS):
        later[i][1]()
        gather_pitched(r2, scr, part)

    @pl.loop(0, 16)
    def _(q):
        for t in range(6):
            hi, lo = split(scr[t, pl.ds(pl.multiple_of(q * PITCH, 8), 48), :])
            rows = pl.ds(pl.multiple_of(q * 48, 16), 48)
            dh[rows, pl.ds(t * 128, 128)] = hi
            dl[rows, pl.ds(t * 128, 128)] = lo

    for out, _in in moves:
        out()
    moves_a = []
    for part in DA_PARTS:
        rows = rows_of(part)

        @pl.loop(0, 3)
        def _(n):
            lanes = pl.ds(pl.multiple_of(n * 256, 256), 256)
            res[rows, lanes] = dot3((bh[rows, :], bl[rows, :]), (dh[:, lanes], dl[:, lanes]), NN)

        spread_rows(res, s1, part)
        moves_a.append(send(s1, r1, part))
    for out, _in in later:
        out()
    moves_b = []
    for part in DB_PARTS:
        rows = rows_of(part)

        @pl.loop(0, 3)
        def _(n):
            lanes = pl.ds(pl.multiple_of(n * 256, 256), 256)
            res[rows, lanes] = dot3((ah[rows, :], al[rows, :]), (dh[lanes, :], dl[lanes, :]), NT)

        spread_rows(res, s2, part)
        moves_b.append(send(s2, r3, part))

    def back(n, lanes, d_ref, lin_ref, sig_ref):
        sig = sig_ref[:, lanes]
        d_lin = d_ref[:, lanes] * mask_ref[:, lanes] * sig
        first = use(n, lanes, d_lin)
        return first + use(n + 1, lanes, d_lin * lin_ref[:, lanes] * (1.0 - sig))

    for i, part in enumerate(DA_PARTS):
        moves_a[i][1]()

        @chunks_of(part)
        def _(s):
            lanes = wide(s)
            sg[:, lanes] += back(0, lanes, r1, la, sa)

    for i, part in enumerate(DB_PARTS):
        moves_b[i][1]()

        @chunks_of(part)
        def _(s):
            lanes = wide(s)
            total = sg[:, lanes] + back(2, lanes, r3, lb, sb)
            hat = hat_ref[:, lanes]
            prod = total * hat
            g1_ref[...] += sum(prod[:, 128 * t : 128 * t + 128] for t in range(6))
            grad = norm_back(total * gain_in, hat, inv_ref[:, lanes]).T
            flat = xin.at[s].reshape(768, 128)
            for j in range(8):
                flat[pl.ds(j, 96, stride=8), :] = grad[j * 96 : (j + 1) * 96, :]
            pltpu.make_async_copy(xin.at[s], gp_hbm.at[:, s], out_sem.at[s]).start()

    for out, _in in moves_a + moves_b:
        out()
    for s in range(6):
        pltpu.make_async_copy(xin.at[s], gp_hbm.at[:, s], out_sem.at[s]).wait()


def whole_step(pair4, go4, mask, gains_t, weights):
    vmem = pl.BlockSpec(memory_space=pltpu.VMEM)
    hbm = pl.BlockSpec(memory_space=pl.ANY)
    full = pltpu.VMEM((128, 4608), F32)
    half = pltpu.VMEM((128, 4608), BF16)
    mat = pltpu.VMEM((768, 768), BF16)
    wts = pltpu.VMEM((768, 128), BF16)
    tiles = pltpu.VMEM((6, 96, 8, 128), F32)
    dma = pltpu.SemaphoreType.DMA
    square = jax.ShapeDtypeStruct((128, 128), F32)
    return pl.pallas_call(
        step_kernel,
        in_specs=[hbm, hbm, vmem, vmem, vmem],
        out_specs=[hbm, vmem, vmem, vmem, vmem],
        out_shape=[
            jax.ShapeDtypeStruct((96, 6, 8, 128), F32),
            jax.ShapeDtypeStruct((640, 128), F32),
            square,
            square,
            square,
        ],
        scratch_shapes=[tiles, tiles, full, full, full, full, full, full]
        + [pltpu.VMEM((1, 4608), F32), half, half]
        + [full] * 6
        + [mat] * 6
        + [pltpu.VMEM((768, 768), F32), pltpu.VMEM((6, 16 * PITCH, 128), F32)]
        + [wts] * 4
        + [pltpu.VMEM((381, 12, 128), F32)]
        + [dma((6,)), dma((6,)), dma((6,)), dma((SENDS,)), dma((SENDS,))],
        compiler_params=params(collective_id=0, has_side_effects=True),
        name="whole_step",
    )(pair4, go4, mask, gains_t, weights)


def on_device(pair_act, grad_out, residue_mask, norm_gains, weights):
    tile_rows, tile_cols, channels = pair_act.shape
    residues = residue_mask.shape[0]
    row_mask = lax.dynamic_slice_in_dim(
        residue_mask, lax.axis_index("row") * tile_rows, tile_rows
    )
    col_mask = lax.dynamic_slice_in_dim(
        residue_mask, lax.axis_index("col") * tile_cols, tile_cols
    )
    mask = (col_mask[:, None] * row_mask[None, :]).astype(F32).reshape(1, -1)
    gains_t = norm_gains.T
    pair4 = pair_act.reshape(tile_rows, tile_cols // 8, 8, channels)
    go4 = grad_out.reshape(tile_rows, tile_cols // 8, 8, channels)
    grad_pair, weight_part, out_part, gain_one, gain_two = whole_step(
        pair4, go4, mask, gains_t, weights
    )
    gains = jnp.stack([gain_one, gain_two]).sum(-1)
    spare = jnp.zeros((1024 - 6 * channels - 2, channels), F32)
    combined = jnp.concatenate([weight_part, out_part, gains, spare], axis=0)
    total = sum_everywhere(1, combined) / residues
    return (
        grad_pair.reshape(pair_act.shape),
        total[: 6 * channels].reshape(6, channels, channels),
        total[6 * channels : 6 * channels + 2],
    )


def solution(mesh):
    return jax.shard_map(
        on_device,
        mesh=mesh,
        in_specs=(P("row", "col", None), P("row", "col", None), P(), P(), P()),
        out_specs=(P("row", "col", None), P(), P()),
        check_vma=False,
    )
```

time: 311 us -> 227 us (0.73)
  Pallas kernels: 294 us -> 215 us
  local copies, waits for them, and re-layouts: 11.4 us -> 6.46 us
    pallas_call x9 -> x1, Pallas kernels: 269 us -> 189 us  [whole_step(): pl.pallas_call(step_kernel, in_specs=[hbm, hbm, vmem, vmem, vmem], out_sp...]
    slice x8 -> x0, local copies, waits for them, and re-layouts: 5.13 us -> none  [the longest x1 0.69 us: on_device(): wl[:cut]]
where the time goes in v2:
time: 227 us; the launch traced here: 226 us
  Pallas kernels  215 us (95%)
  local copies, waits for them, and re-layouts  6.46 us (3%)
  other arithmetic  4.3 us (2%)
    pallas_call x1, Pallas kernels, whole_step(): pl.pallas_call(step_kernel, in_specs=[hbm, hbm, vmem, vmem, vmem], out_sp...  189 us
    pallas_call x1, Pallas kernels, sum_everywhere(): pl.pallas_call(sum_kernel, out_shape=jax.ShapeDtypeStruct(x.shape, x.dtyp...  25.9 us

profile of v2, /device:TPU:1, one launch (start us, length us, event | category | flops | bytes accessed | tf_op | source)
XLA Modules:
  0.0 226.3 jit_solution(12606925528580478453)
XLA Ops:
  0.6 0.8 dynamic_slice.6
  1.4 0.8 dynamic_slice.7
  2.2 0.1 multiply_convert_fusion
  2.2 0.7 convert_element_type.14.mask_ref
  2.9 1.4 copy.8
  4.3 189.0 %whole_step.1 = (f32[96,6,8,128]{3,2,1,0:T(8,128)}, f32[640,128]{1,0:T(8,128)}, f32[128,128]{1,0:T(8,128)}, f32[128,128]{1,0:T(8,128)}, f32[128,128]{1,0:T(8,128)}) custom-call(f32[96,6,8,128]{3,2,1,0:T(8,128)} %bitcast.7, f32[96,6,8,128]{3,2,1,0:T(8,128)} %bitcast.8, f32[1,4608]{1,0:T(1,128)} %convert_element_type.14.mask_ref, f32[128,2]{1,0:T(8,128)} %bitcast.11, ...), custom_call_target="tpu_custom_call" | custom-call | tf_op jit(solution)/shard_map/whole_step/pallas_call | solution.py:508
  193.4 0.0 copy-start
  193.4 1.1 maximum_reduce_fusion
  194.5 0.1 pad.3.clone
  194.6 2.0 maximum_maximum_fusion.x_ref
  196.6 25.9 %sum_everywhere.1 = f32[1024,128]{1,0:T(8,128)} custom-call(f32[1024,128]{1,0:T(8,128)} %maximum_maximum_fusion.x_ref), custom_call_target="tpu_custom_call" | custom-call | tf_op jit(solution)/shard_map/sum_everywhere/pallas_call | solution.py:137
  222.5 1.1 broadcast_multiply_fusion
  223.6 0.8 slice.8
  224.3 0.6 slice.9
  224.9 0.0 copy-done
  224.9 1.4 copy.10
  (1 shorter events, 0.0 us)
Async XLA Ops:
  193.4 31.5 %copy-start = (f32[96,6,8,128]{3,2,1,0:T(8,128)S(1)}, f32[96,6,8,128]{3,2,1,0:T(8,128)}, u32[]{:S(2)}) copy-start(f32[96,6,8,128]{3,2,1,0:T(8,128)} %get-tuple-element.8) | copy-start | bytes 7077892

commit v3 on v2

--- a/solution.py
+++ b/solution.py
@@ -86,64 +86,50 @@
     pltpu.make_async_copy(some, some, sem).wait()
 
 
-def sum_kernel(x_ref, out_ref, parts, mine, send_a, recv_a, send_b, recv_b):
-    spot = place()
-    me = lax.axis_index("row") * 16 + lax.axis_index("col")
-    barrier = pltpu.get_barrier_semaphore()
-    for step in steps():
-        r, q = partner(spot, step)
-        pl.semaphore_signal(
-            barrier, inc=1, device_id={"row": r, "col": q}, device_id_type=MESH
-        )
-    pl.semaphore_wait(barrier, 127)
-
-    def rows_of(owner):
-        return pl.ds(pl.multiple_of(owner * 8, 8), 8)
-
-    for step in steps():
-        r, q = partner(spot, step)
-        to = r * 16 + q
-        pltpu.make_async_remote_copy(
-            src_ref=x_ref.at[rows_of(to), :],
-            dst_ref=parts.at[rows_of(me), :],
-            send_sem=send_a,
-            recv_sem=recv_a,
-            device_id={"row": r, "col": q},
-            device_id_type=MESH,
-        ).start()
-    pltpu.make_async_copy(x_ref.at[rows_of(me), :], parts.at[rows_of(me), :], recv_a).start()
-    pltpu.make_async_copy(x_ref, parts, recv_a).wait()
-    total = parts[...].reshape(128, 8, 128).sum(0)
-    mine[...] = total
-    for step in steps():
-        r, q = partner(spot, step)
-        pltpu.make_async_remote_copy(
-            src_ref=mine,
-            dst_ref=out_ref.at[rows_of(me), :],
-            send_sem=send_b,
-            recv_sem=recv_b,
-            device_id={"row": r, "col": q},
-            device_id_type=MESH,
-        ).start()
-    pltpu.make_async_copy(mine, out_ref.at[rows_of(me), :], recv_b).start()
-    pltpu.make_async_copy(x_ref, out_ref, recv_b).wait()
-    some = x_ref.at[pl.ds(0, 127 * 8), :]
-    into = parts.at[pl.ds(0, 127 * 8), :]
-    pltpu.make_async_copy(some, into, send_a).wait()
-    pltpu.make_async_copy(some, into, send_b).wait()
-
-
-def sum_everywhere(ident, x):
-    return pl.pallas_call(
-        sum_kernel,
-        out_shape=jax.ShapeDtypeStruct(x.shape, x.dtype),
-        in_specs=[pl.BlockSpec(memory_space=pl.ANY)],
-        out_specs=pl.BlockSpec(memory_space=pl.ANY),
-        scratch_shapes=[pltpu.VMEM((1024, 128), F32), pltpu.VMEM((8, 128), F32)]
-        + [pltpu.SemaphoreType.DMA] * 4,
-        compiler_params=params(collective_id=ident, has_side_effects=True),
-        name="sum_everywhere",
-    )(x)
+def chip_at(spot, a, b, c):
+    x, y, z, _ = spot
+    return lax.rem(x + a, 4), lax.rem(y + b, 4), lax.rem(z + c, 4)
+
+
+def device_at(x, y, z, core):
+    return x * 2 + z // 2, y * 4 + lax.rem(z, 2) * 2 + core
+
+
+def eight(tile):
+    return pl.ds(pl.multiple_of(tile * 8, 8), 8)
+
+
+def tile_copy(src, dst, send_sem, recv_sem, device):
+    return pltpu.make_async_remote_copy(
+        src_ref=src,
+        dst_ref=dst,
+        send_sem=send_sem,
+        recv_sem=recv_sem,
+        device_id={"row": device[0], "col": device[1]},
+        device_id_type=MESH,
+    )
+
+
+def wait_tiles(ref, count, sem):
+    some = ref.at[pl.ds(0, count * 8), :]
+    pltpu.make_async_copy(some, some, sem).wait()
+
+
+def settle(small, large, tiles, owner, send_sem, recv_sem, n):
+    @pl.when(owner)
+    def _():
+        if tiles > 1:
+            wait_tiles(small, tiles - 1, send_sem.at[n])
+            wait_tiles(small, tiles - 1, recv_sem.at[n + 1])
+        wait_tiles(large, 127, send_sem.at[n + 1])
+
+    @pl.when(jnp.logical_not(owner))
+    def _():
+        wait_tiles(small, tiles, send_sem.at[n])
+        wait_tiles(small, tiles, recv_sem.at[n + 1])
+
+
+CHIPS = [(o // 16, o // 4 % 4, o % 4) for o in [(s * 27) % 64 for s in range(64)]]
 
 
 def turn_in(ref):
@@ -197,7 +183,7 @@
 
 
 PITCH = 56
-UNIT = 1536
+UNIT = 768
 
 
 def lanes_of(part):
@@ -205,15 +191,15 @@
 
 
 def groups_of(part):
-    return pl.loop(part[0] * 4, part[1] * 4)
+    return pl.loop(part[0] * 2, part[1] * 2)
 
 
 def chunks_of(part):
-    return pl.loop(part[0] * 2, part[1] * 2)
+    return pl.loop(part[0], part[1])
 
 
 def rows_of(part):
-    return pl.ds(part[0] * 256, (part[1] - part[0]) * 256)
+    return pl.ds(part[0] * 128, (part[1] - part[0]) * 128)
 
 
 def gather_matrix(src_ref, hi_ref, lo_ref, part):
@@ -267,20 +253,21 @@
                     ]
 
 
-A_PARTS = ((0, 2), (2, 3))
-T_PARTS = ((0, 2), (2, 3))
-D_PARTS = ((0, 2), (2, 3))
-DA_PARTS = ((0, 1), (1, 3))
-DB_PARTS = ((0, 2), (2, 3))
-ALL = (0, 3)
-SENDS = 11
+B_PARTS = ((0, 2), (2, 6))
+A_PARTS = ((0, 4), (4, 6))
+T_PARTS = ((0, 2), (2, 4), (4, 6))
+DA_PARTS = ((0, 2), (2, 6))
+DB_PARTS = ((0, 3), (3, 5), (5, 6))
+ALL = (0, 6)
+SENDS = 15
 
 
 def step_kernel(
-    pair_hbm, go_hbm, mask_ref, gain_ref, w_ref, gp_hbm, gw_ref, ow_ref, g1_ref, g2_ref,
+    pair_hbm, go_hbm, valid_ref, gain_ref, w_ref, gp_hbm, wo_ref, go_ref,
     xin, gin, s1, s2, r1, r2, r3, hat_ref, inv_ref, nh, nl, la, sa, lb, sb, sg, dg,
     ah, al, bh, bl, dh, dl, res, scr, th, tl, uh, ul, tally,
-    in_sem, go_sem, out_sem, send_sem, recv_sem,
+    mask_ref, gw_ref, g1_ref, g2_ref, gains, parts1, parts2, mine,
+    in_sem, go_sem, out_sem, send_sem, recv_sem, sum_send, sum_recv,
 ):
     spot = place()
     for s in range(6):
@@ -298,11 +285,27 @@
         th[rows, :], tl[rows, :] = split(w_ref[n].T)
         uh[rows, :], ul[rows, :] = split(w_ref[n])
     gw_ref[...] = jnp.zeros_like(gw_ref)
-    ow_ref[...] = jnp.zeros_like(ow_ref)
     g1_ref[...] = jnp.zeros_like(g1_ref)
     g2_ref[...] = jnp.zeros_like(g2_ref)
-    gain_in = gain_ref[:, 0:1]
-    gain_tri = gain_ref[:, 1:2]
+    for n in range(2):
+        gains[n] = jnp.broadcast_to(gain_ref[n : n + 1, :], (128, 128)).T
+    gain_in = gains[0, :, 0:1]
+    gain_tri = gains[1, :, 0:1]
+    me = lax.axis_index("row") * 16 + lax.axis_index("col")
+    x, y, z, core = spot
+    first_row = lax.axis_index("row") * 96
+    first_col = lax.axis_index("col") * 48
+    lane = lax.broadcasted_iota(jnp.int32, (1, 768), 1)
+    in_row = lax.rem(lane, 96)
+    in_col = lane // 96
+    row_valid = jnp.zeros((1, 768), jnp.int32)
+    for i in range(96):
+        row_valid = jnp.where(in_row == i, valid_ref[first_row + i], row_valid)
+    for s in range(6):
+        col_valid = jnp.zeros((1, 768), jnp.int32)
+        for j in range(8):
+            col_valid = jnp.where(in_col == j, valid_ref[first_col + s * 8 + j], col_valid)
+        mask_ref[:, s * 768 : s * 768 + 768] = (row_valid * col_valid).astype(F32)
 
     def wide(s):
         return pl.ds(pl.multiple_of(s * 768, 768), 768)
@@ -319,17 +322,6 @@
         sig_ref[:, lanes] = sig
         out_ref[:, lanes] = mask_ref[:, lanes] * sig * lin
 
-    @chunks_of(ALL)
-    def _(s):
-        lanes = wide(s)
-        pltpu.make_async_copy(pair_hbm.at[:, s], xin.at[s], in_sem.at[s]).wait()
-        hat, inv = norm_parts(turn_in(xin.at[s]))
-        hat_ref[:, lanes] = hat
-        inv_ref[:, lanes] = inv
-        nh[:, lanes], nl[:, lanes] = split(hat * gain_in)
-        side(2, lanes, lb, sb, s2)
-
-    pl.semaphore_wait(barrier, 127)
     which = iter(range(SENDS))
 
     def send(src, dst, part):
@@ -341,7 +333,22 @@
             lambda: wait_all(tally, part, recv_sem.at[n]),
         )
 
-    b_out, b_in = send(s2, r2, ALL)
+    moves_r = []
+    for i, part in enumerate(B_PARTS):
+
+        @chunks_of(part)
+        def _(s):
+            lanes = wide(s)
+            pltpu.make_async_copy(pair_hbm.at[:, s], xin.at[s], in_sem.at[s]).wait()
+            hat, inv = norm_parts(turn_in(xin.at[s]))
+            hat_ref[:, lanes] = hat
+            inv_ref[:, lanes] = inv
+            nh[:, lanes], nl[:, lanes] = split(hat * gain_in)
+            side(2, lanes, lb, sb, s2)
+
+        if i == 0:
+            pl.semaphore_wait(barrier, 127)
+        moves_r.append(send(s2, r2, part))
     moves = []
     for part in A_PARTS:
 
@@ -356,8 +363,9 @@
         lanes = wide(s)
         sg[:, lanes] = sigmoid(dot3(weight(4), (nh[:, lanes], nl[:, lanes]), NN))
 
-    b_in()
-    gather_matrix(r2, bh, bl, ALL)
+    for i, part in enumerate(B_PARTS):
+        moves_r[i][1]()
+        gather_matrix(r2, bh, bl, part)
     for i, part in enumerate(A_PARTS):
         moves[i][1]()
         gather_matrix(r1, ah, al, part)
@@ -385,9 +393,10 @@
         spread_pitched(scr, s1, part)
         moves.append(send(s1, r3, part))
 
-    b_out()
+    for out, _in in moves_r:
+        out()
     later = []
-    for i, part in enumerate(D_PARTS):
+    for i, part in enumerate(T_PARTS):
         moves[i][1]()
 
         @chunks_of(part)
@@ -403,7 +412,7 @@
             d_out = split(d_out)
             d_norm = dot3(weight(5, uh, ul), d_out, NN)
             s2[:, lanes] = norm_back(d_norm * gain_tri, tri_hat, tri_inv)
-            ow_ref[...] += dot3(tri_norm, d_out, NT)
+            gw_ref[pl.ds(640, 128), :] += dot3(tri_norm, d_out, NT)
             prod = d_norm * tri_hat
             g2_ref[...] += sum(prod[:, 128 * t : 128 * t + 128] for t in range(6))
 
@@ -420,17 +429,18 @@
         lanes = wide(s)
         sg[:, lanes] = use(4, lanes, dg[:, lanes])
 
-    for i, part in enumerate(D_PARTS):
+    for i, part in enumerate(T_PARTS):
         later[i][1]()
         gather_pitched(r2, scr, part)
-
-    @pl.loop(0, 16)
-    def _(q):
-        for t in range(6):
-            hi, lo = split(scr[t, pl.ds(pl.multiple_of(q * PITCH, 8), 48), :])
-            rows = pl.ds(pl.multiple_of(q * 48, 16), 48)
-            dh[rows, pl.ds(t * 128, 128)] = hi
-            dl[rows, pl.ds(t * 128, 128)] = lo
+        first, many = part[0] * 8, (part[1] - part[0]) * 8
+
+        @pl.loop(0, 16)
+        def _(q):
+            for t in range(6):
+                hi, lo = split(scr[t, pl.ds(pl.multiple_of(q * PITCH + first, 8), many), :])
+                rows = pl.ds(pl.multiple_of(q * 48 + first, 16), many)
+                dh[rows, pl.ds(t * 128, 128)] = hi
+                dl[rows, pl.ds(t * 128, 128)] = lo
 
     for out, _in in moves:
         out()
@@ -473,8 +483,78 @@
             lanes = wide(s)
             sg[:, lanes] += back(0, lanes, r1, la, sa)
 
+    def source_row(tile):
+        return tile * 8 + (tile // 32) * 256
+
+    def early_tile(x, y, z):
+        return (x * 4 + y) * 4 + z
+
+    for a, b, c in CHIPS:
+        tx, ty, tz = chip_at(spot, a, b, c)
+        rows = pl.ds(pl.multiple_of(source_row(early_tile(tx, ty, tz)), 8), 8)
+        copy = tile_copy(
+            gw_ref.at[rows, :], parts1.at[eight(me), :], sum_send.at[0], sum_recv.at[0],
+            device_at(tx, ty, tz, 0),
+        )
+        if (a, b, c) == (0, 0, 0):
+            pl.when(core == 1)(copy.start)
+        else:
+            copy.start()
+
+    early_rows = pl.ds(pl.multiple_of(source_row(early_tile(x, y, z)), 8), 8)
+
+    def reduce_tile(src_rows, parts, out_ref, out_rows, n):
+        parts[eight(me), :] = gw_ref[src_rows, :]
+        wait_tiles(parts, 127, sum_recv.at[n])
+        total = parts[...].reshape(128, 8, 128).sum(0) * (1.0 / 768)
+        mine[...] = total
+        out_ref[out_rows, :] = total
+        for step in steps():
+            tile_copy(
+                mine, out_ref.at[out_rows, :], sum_send.at[n + 1], sum_recv.at[n + 1],
+                partner(spot, step),
+            ).start()
+
+    def early_reduce():
+        @pl.when(core == 0)
+        def _():
+            reduce_tile(early_rows, parts1, wo_ref, early_rows, 0)
+
+    late_z = (z // 2) * 2
+    late_owner = jnp.logical_and(core == 1, lax.rem(z, 2) == 0)
+    gain_x, gain_y, gain_z, gain_core = 0, 0, 1, 1
+    gain_device = device_at(gain_x, gain_y, gain_z, gain_core)
+    gain_me = gain_device[0] * 16 + gain_device[1]
+    gain_owner = me == gain_me
+
+    def late_row(x, y, z):
+        return pl.multiple_of(256 + ((x * 4 + y) * 2 + z // 2) * 8, 8)
+
+    def late_send():
+        for a, b, c in CHIPS:
+            if c % 2:
+                continue
+            tx, ty, tz = lax.rem(x + a, 4), lax.rem(y + b, 4), lax.rem(late_z + c, 4)
+            copy = tile_copy(
+                gw_ref.at[pl.ds(late_row(tx, ty, tz), 8), :], parts2.at[eight(me), :],
+                sum_send.at[2], sum_recv.at[2], device_at(tx, ty, tz, 1),
+            )
+            if (a, b, c) == (0, 0, 0):
+                pl.when(jnp.logical_not(late_owner))(copy.start)
+            else:
+                copy.start()
+        for n, ref in ((0, g1_ref), (1, g2_ref)):
+            gw_ref[pl.ds(768 + n, 1), :] = jnp.sum(ref[...].T, axis=0, keepdims=True)
+        pl.when(jnp.logical_not(gain_owner))(
+            tile_copy(
+                gw_ref.at[pl.ds(768, 8), :], parts2.at[eight(me), :],
+                sum_send.at[4], sum_recv.at[4], gain_device,
+            ).start
+        )
+
     for i, part in enumerate(DB_PARTS):
         moves_b[i][1]()
+        last = i == len(DB_PARTS) - 1
 
         @chunks_of(part)
         def _(s):
@@ -483,19 +563,44 @@
             hat = hat_ref[:, lanes]
             prod = total * hat
             g1_ref[...] += sum(prod[:, 128 * t : 128 * t + 128] for t in range(6))
-            grad = norm_back(total * gain_in, hat, inv_ref[:, lanes]).T
+            sg[:, lanes] = total
+
+        if last:
+            late_send()
+
+        @chunks_of(part)
+        def _(s):
+            lanes = wide(s)
+            grad = norm_back(sg[:, lanes] * gain_in, hat_ref[:, lanes], inv_ref[:, lanes]).T
             flat = xin.at[s].reshape(768, 128)
             for j in range(8):
                 flat[pl.ds(j, 96, stride=8), :] = grad[j * 96 : (j + 1) * 96, :]
             pltpu.make_async_copy(xin.at[s], gp_hbm.at[:, s], out_sem.at[s]).start()
 
+        if i == 0:
+            early_reduce()
+
+    late_rows = pl.ds(late_row(x, y, late_z), 8)
+
+    @pl.when(late_owner)
+    def _():
+        reduce_tile(late_rows, parts2, wo_ref, late_rows, 2)
+
+    @pl.when(gain_owner)
+    def _():
+        reduce_tile(pl.ds(768, 8), parts2, go_ref, pl.ds(0, 8), 4)
+
     for out, _in in moves_a + moves_b:
         out()
     for s in range(6):
         pltpu.make_async_copy(xin.at[s], gp_hbm.at[:, s], out_sem.at[s]).wait()
 
-
-def whole_step(pair4, go4, mask, gains_t, weights):
+    settle(gw_ref, parts1, 64, core == 0, sum_send, sum_recv, 0)
+    settle(gw_ref, parts1, 32, late_owner, sum_send, sum_recv, 2)
+    settle(gw_ref, parts1, 1, gain_owner, sum_send, sum_recv, 4)
+
+
+def whole_step(pair4, go4, valid, gains, weights):
     vmem = pl.BlockSpec(memory_space=pltpu.VMEM)
     hbm = pl.BlockSpec(memory_space=pl.ANY)
     full = pltpu.VMEM((128, 4608), F32)
@@ -504,17 +609,15 @@
     wts = pltpu.VMEM((768, 128), BF16)
     tiles = pltpu.VMEM((6, 96, 8, 128), F32)
     dma = pltpu.SemaphoreType.DMA
-    square = jax.ShapeDtypeStruct((128, 128), F32)
+    square = pltpu.VMEM((128, 128), F32)
     return pl.pallas_call(
         step_kernel,
-        in_specs=[hbm, hbm, vmem, vmem, vmem],
-        out_specs=[hbm, vmem, vmem, vmem, vmem],
+        in_specs=[hbm, hbm, pl.BlockSpec(memory_space=pltpu.SMEM), vmem, vmem],
+        out_specs=[hbm, vmem, vmem],
         out_shape=[
             jax.ShapeDtypeStruct((96, 6, 8, 128), F32),
-            jax.ShapeDtypeStruct((640, 128), F32),
-            square,
-            square,
-            square,
+            jax.ShapeDtypeStruct((768, 128), F32),
+            jax.ShapeDtypeStruct((8, 128), F32),
         ],
         scratch_shapes=[tiles, tiles, full, full, full, full, full, full]
         + [pltpu.VMEM((1, 4608), F32), half, half]
@@ -522,37 +625,29 @@
         + [mat] * 6
         + [pltpu.VMEM((768, 768), F32), pltpu.VMEM((6, 16 * PITCH, 128), F32)]
         + [wts] * 4
-        + [pltpu.VMEM((381, 12, 128), F32)]
-        + [dma((6,)), dma((6,)), dma((6,)), dma((SENDS,)), dma((SENDS,))],
+        + [pltpu.VMEM((762, 6, 128), F32)]
+        + [pltpu.VMEM((1, 4608), F32), pltpu.VMEM((776, 128), F32), square, square]
+        + [pltpu.VMEM((2, 128, 128), F32)]
+        + [pltpu.VMEM((1024, 128), F32)] * 2
+        + [pltpu.VMEM((8, 128), F32)]
+        + [dma((6,)), dma((6,)), dma((6,)), dma((SENDS,)), dma((SENDS,))]
+        + [dma((6,)), dma((6,))],
         compiler_params=params(collective_id=0, has_side_effects=True),
         name="whole_step",
-    )(pair4, go4, mask, gains_t, weights)
+    )(pair4, go4, valid, gains, weights)
 
 
 def on_device(pair_act, grad_out, residue_mask, norm_gains, weights):
     tile_rows, tile_cols, channels = pair_act.shape
-    residues = residue_mask.shape[0]
-    row_mask = lax.dynamic_slice_in_dim(
-        residue_mask, lax.axis_index("row") * tile_rows, tile_rows
-    )
-    col_mask = lax.dynamic_slice_in_dim(
-        residue_mask, lax.axis_index("col") * tile_cols, tile_cols
-    )
-    mask = (col_mask[:, None] * row_mask[None, :]).astype(F32).reshape(1, -1)
-    gains_t = norm_gains.T
     pair4 = pair_act.reshape(tile_rows, tile_cols // 8, 8, channels)
     go4 = grad_out.reshape(tile_rows, tile_cols // 8, 8, channels)
-    grad_pair, weight_part, out_part, gain_one, gain_two = whole_step(
-        pair4, go4, mask, gains_t, weights
+    grad_pair, grad_weights, grad_gains = whole_step(
+        pair4, go4, residue_mask, norm_gains, weights
     )
-    gains = jnp.stack([gain_one, gain_two]).sum(-1)
-    spare = jnp.zeros((1024 - 6 * channels - 2, channels), F32)
-    combined = jnp.concatenate([weight_part, out_part, gains, spare], axis=0)
-    total = sum_everywhere(1, combined) / residues
     return (
         grad_pair.reshape(pair_act.shape),
-        total[: 6 * channels].reshape(6, channels, channels),
-        total[6 * channels : 6 * channels + 2],
+        grad_weights.reshape(weights.shape),
+        grad_gains[: norm_gains.shape[0]],
     )
 
 

time: 227 us -> 211 us (0.930)
  Pallas kernels: 215 us -> 205 us
  other arithmetic: 4.3 us -> 0 us
    pallas_call x2 -> x1, Pallas kernels: 215 us -> 205 us  [whole_step(): pl.pallas_call(step_kernel, in_specs=[hbm, hbm, pl.BlockSpec(memory_space...]
where the time goes in v3:
time: 211 us
  Pallas kernels  205 us (97%)
  local copies, waits for them, and re-layouts  5.27 us (2%)
    pallas_call x1, Pallas kernels, whole_step(): pl.pallas_call(step_kernel, in_specs=[hbm, hbm, pl.BlockSpec(memory_space...  205 us

profile of v3, /device:TPU:1, one launch (start us, length us, event | category | flops | bytes accessed | tf_op | source)
XLA Modules:
  0.0 210.9 jit_solution(15393910367441818023)
XLA Ops:
  0.6 205.0 %whole_step.1 = (f32[96,6,8,128]{3,2,1,0:T(8,128)}, f32[768,128]{1,0:T(8,128)}, f32[8,128]{1,0:T(8,128)}) custom-call(f32[96,6,8,128]{3,2,1,0:T(8,128)} %bitcast.4, f32[96,6,8,128]{3,2,1,0:T(8,128)} %bitcast.5, s32[768]{0:T(1024)} %valid_ref.1, f32[2,128]{1,0:T(2,128)} %gain_ref.1, f32[6,128,128]{2,1,0:T(8,128)} %w_ref.1), custom_call_target="tpu_custom_call" | custom-call | tf_op jit(solution)/shard_map/whole_step/pallas_call | solution.py:613
  205.6 1.2 slice.3
  206.9 0.0 copy-start
  206.9 3.3 %copy.10 = f32[96,48,128]{2,1,0:T(8,128)} copy(f32[96,48,128]{2,1,0:T(8,128)} %bitcast.6) | data formatting | bytes 4718592
  210.2 0.0 copy-done
  210.2 0.7 copy.11
Async XLA Ops:
  206.9 3.3 %copy-start = (f32[768,128]{1,0:T(8,128)S(1)}, f32[768,128]{1,0:T(8,128)}, u32[]{:S(2)}) copy-start(f32[768,128]{1,0:T(8,128)} %get-tuple-element.7) | copy-start | bytes 1179652

commit v4 on v3

--- a/solution.py
+++ b/solution.py
@@ -263,10 +263,10 @@
 
 
 def step_kernel(
-    pair_hbm, go_hbm, valid_ref, gain_ref, w_ref, gp_hbm, wo_ref, go_ref,
+    pair_hbm, go_hbm, valid_ref, gain_ref, w_ref, gp_hbm, wo_ref, gains_out,
     xin, gin, s1, s2, r1, r2, r3, hat_ref, inv_ref, nh, nl, la, sa, lb, sb, sg, dg,
-    ah, al, bh, bl, dh, dl, res, scr, th, tl, uh, ul, tally,
-    mask_ref, gw_ref, g1_ref, g2_ref, gains, parts1, parts2, mine,
+    ah, al, bh, bl, th_b, tl_b, dh, dl, res, scr, th, tl, uh, ul, tally,
+    mask_ref, gw_ref, g1_ref, g2_ref, gains, parts1, parts2, mine, go_ref,
     in_sem, go_sem, out_sem, send_sem, recv_sem, sum_send, sum_recv,
 ):
     spot = place()
@@ -280,10 +280,13 @@
         pl.semaphore_signal(
             barrier, inc=1, device_id={"row": r, "col": q}, device_id_type=MESH
         )
-    for n in range(6):
+    def prepare(n):
         rows = pl.ds(n * 128, 128)
         th[rows, :], tl[rows, :] = split(w_ref[n].T)
         uh[rows, :], ul[rows, :] = split(w_ref[n])
+
+    prepare(2)
+    prepare(3)
     gw_ref[...] = jnp.zeros_like(gw_ref)
     g1_ref[...] = jnp.zeros_like(g1_ref)
     g2_ref[...] = jnp.zeros_like(g2_ref)
@@ -349,6 +352,9 @@
         if i == 0:
             pl.semaphore_wait(barrier, 127)
         moves_r.append(send(s2, r2, part))
+        if i == 0:
+            for n in (0, 1, 4, 5):
+                prepare(n)
     moves = []
     for part in A_PARTS:
 
@@ -366,6 +372,15 @@
     for i, part in enumerate(B_PARTS):
         moves_r[i][1]()
         gather_matrix(r2, bh, bl, part)
+
+        @chunks_of(part)
+        def _(s):
+            here = pl.ds(pl.multiple_of(s * 128, 128), 128)
+            for src, out in ((bh, th_b), (bl, tl_b)):
+                for j in range(6):
+                    there = pl.ds(j * 128, 128)
+                    out[there, here] = src[here, there].T
+
     for i, part in enumerate(A_PARTS):
         moves[i][1]()
         gather_matrix(r1, ah, al, part)
@@ -374,7 +389,9 @@
         @pl.loop(0, 3)
         def _(n):
             lanes = pl.ds(pl.multiple_of(n * 256, 256), 256)
-            got = dot3((bh[rows, :], bl[rows, :]), (ah[rows, lanes], al[rows, lanes]), TN)
+            got = dot3(
+                (th_b[:, rows], tl_b[:, rows]), (ah[rows, lanes], al[rows, lanes]), NN
+            )
             if i > 0:
                 got = got + res[:, lanes]
             if i < len(A_PARTS) - 1:
@@ -572,12 +589,11 @@
         def _(s):
             lanes = wide(s)
             grad = norm_back(sg[:, lanes] * gain_in, hat_ref[:, lanes], inv_ref[:, lanes]).T
-            flat = xin.at[s].reshape(768, 128)
+            flat = gp_hbm.at[s].reshape(768, 128)
             for j in range(8):
                 flat[pl.ds(j, 96, stride=8), :] = grad[j * 96 : (j + 1) * 96, :]
-            pltpu.make_async_copy(xin.at[s], gp_hbm.at[:, s], out_sem.at[s]).start()
-
-        if i == 0:
+
+        if last:
             early_reduce()
 
     late_rows = pl.ds(late_row(x, y, late_z), 8)
@@ -592,12 +608,11 @@
 
     for out, _in in moves_a + moves_b:
         out()
-    for s in range(6):
-        pltpu.make_async_copy(xin.at[s], gp_hbm.at[:, s], out_sem.at[s]).wait()
 
     settle(gw_ref, parts1, 64, core == 0, sum_send, sum_recv, 0)
     settle(gw_ref, parts1, 32, late_owner, sum_send, sum_recv, 2)
     settle(gw_ref, parts1, 1, gain_owner, sum_send, sum_recv, 4)
+    gains_out[...] = go_ref[0:2, :]
 
 
 def whole_step(pair4, go4, valid, gains, weights):
@@ -613,23 +628,23 @@
     return pl.pallas_call(
         step_kernel,
         in_specs=[hbm, hbm, pl.BlockSpec(memory_space=pltpu.SMEM), vmem, vmem],
-        out_specs=[hbm, vmem, vmem],
+        out_specs=[vmem, vmem, vmem],
         out_shape=[
-            jax.ShapeDtypeStruct((96, 6, 8, 128), F32),
+            pltpu.VMEM((6, 96, 8, 128), F32),
             jax.ShapeDtypeStruct((768, 128), F32),
-            jax.ShapeDtypeStruct((8, 128), F32),
+            jax.ShapeDtypeStruct((2, 128), F32),
         ],
         scratch_shapes=[tiles, tiles, full, full, full, full, full, full]
         + [pltpu.VMEM((1, 4608), F32), half, half]
         + [full] * 6
-        + [mat] * 6
+        + [mat] * 8
         + [pltpu.VMEM((768, 768), F32), pltpu.VMEM((6, 16 * PITCH, 128), F32)]
         + [wts] * 4
         + [pltpu.VMEM((762, 6, 128), F32)]
         + [pltpu.VMEM((1, 4608), F32), pltpu.VMEM((776, 128), F32), square, square]
         + [pltpu.VMEM((2, 128, 128), F32)]
         + [pltpu.VMEM((1024, 128), F32)] * 2
-        + [pltpu.VMEM((8, 128), F32)]
+        + [pltpu.VMEM((8, 128), F32)] * 2
         + [dma((6,)), dma((6,)), dma((6,)), dma((SENDS,)), dma((SENDS,))]
         + [dma((6,)), dma((6,))],
         compiler_params=params(collective_id=0, has_side_effects=True),
@@ -645,9 +660,9 @@
         pair4, go4, residue_mask, norm_gains, weights
     )
     return (
-        grad_pair.reshape(pair_act.shape),
+        jnp.transpose(grad_pair, (1, 0, 2, 3)).reshape(pair_act.shape),
         grad_weights.reshape(weights.shape),
-        grad_gains[: norm_gains.shape[0]],
+        grad_gains,
     )
 
 

time: 211 us -> 204 us (0.967)
  Pallas kernels: 205 us -> 200 us
  local copies, waits for them, and re-layouts: 5.27 us -> 2.9 us
    pallas_call x1, Pallas kernels: 205 us -> 200 us  [whole_step(): pl.pallas_call(step_kernel, in_specs=[hbm, hbm, pl.BlockSpec(memory_space...]
    unnamed x4 -> x6, local copies, waits for them, and re-layouts: 4.02 us -> 1.32 us
where the time goes in v4:
time: 204 us
  Pallas kernels  200 us (98%)
  local copies, waits for them, and re-layouts  2.9 us (1%)
    pallas_call x1, Pallas kernels, whole_step(): pl.pallas_call(step_kernel, in_specs=[hbm, hbm, pl.BlockSpec(memory_space...  200 us

profile of v4, /device:TPU:1, one launch (start us, length us, event | category | flops | bytes accessed | tf_op | source)
XLA Modules:
  0.0 204.0 jit_solution(7073758458425517969)
XLA Ops:
  0.6 200.4 %whole_step.1 = (f32[6,96,8,128]{3,2,1,0:T(8,128)S(1)}, f32[768,128]{1,0:T(8,128)}, f32[2,128]{1,0:T(2,128)}) custom-call(f32[96,6,8,128]{3,2,1,0:T(8,128)} %bitcast.8, f32[96,6,8,128]{3,2,1,0:T(8,128)} %bitcast.9, s32[768]{0:T(1024)} %valid_ref.1, f32[2,128]{1,0:T(2,128)} %gain_ref.1, f32[6,128,128]{2,1,0:T(8,128)} %w_ref.1), custom_call_target="tpu_custom_call" | custom-call | tf_op jit(solution)/shard_map/whole_step/pallas_call | solution.py:628
  201.1 0.0 copy-start
  201.1 0.0 copy-start.1
  201.1 1.6 copy_bitcast_fusion
  202.7 0.0 copy-done
  202.7 0.7 copy.12
  203.4 0.0 copy-done.1
  203.4 0.6 copy.13
Async XLA Ops:
  201.1 1.6 copy-start
  201.1 2.3 %copy-start.1 = (f32[2,128]{1,0:T(2,128)S(1)}, f32[2,128]{1,0:T(2,128)}, u32[]{:S(2)}) copy-start(f32[2,128]{1,0:T(2,128)} %get-tuple-element.14) | copy-start | bytes 3076
